TPU v7x, 256 devices: a whole 4x4x8 slice. The times are simulated.
256 devices in a mesh: px: 32 (over x, z_hi, core), py: 8 (over z_lo, y).
Axes of the slice: x: 4, y: 4, z: 8 (z_hi: 4, z_lo: 2; z = z_hi * 2 + z_lo), core: 2. Of those that a mesh axis runs over, the one named last changes fastest.
Arguments:
- velocity: float32 [3, 1024, 8, 1024], P(None, 'px', 'py'), may hold values from -1.5 to 2.5
- band_of: int32 [8], replicated, may hold values from 0 to 1, as said below
Outputs:
- correlation: float32 [6, 2, 1024, 1024], P(None, None, ('px', 'py'))
Inputs may be any that keep to these rules, and one draw needn't show every extreme that they name: `band_of`: every band 0 to 1 holds at least one plane.
All inputs are finite; a program needn't handle non-finite values.
Results may differ from a plain program's by a relative error of at most 0.00013.
Values sent between devices are 32-bit elements; how exact they have to be, the bound alone decides.
No kernel may reach another device: no remote copies, remote signals or barrier semaphores. Data moves between devices by JAX's collectives and lax.ppermute only.
A program may use at most 64 MiB of HBM per device.

v0:
```python
import math

import jax
import jax.numpy as jnp
import numpy as np
from jax import lax
from jax.experimental import pallas as pl
from jax.experimental.pallas import tpu as pltpu
from jax.sharding import PartitionSpec as P

NX = 1024
NZ = 1024
NY = 8
NB = 2
PAIR_LIST = ((0, 0), (0, 1), (0, 2), (1, 1), (1, 2), (2, 2))
ROOT_HALF = math.sqrt(0.5)
F32 = jnp.float32
BF16 = jnp.bfloat16


def wave(rows, cols, length):
    angle = 2.0 * np.pi * (np.multiply.outer(rows, cols) % length) / length
    return np.cos(angle), np.sin(angle)


def stacked_split(table):
    high = table.astype(np.float32).astype(jnp.bfloat16)
    low = (table - high.astype(np.float64)).astype(np.float32).astype(jnp.bfloat16)
    return np.concatenate((high, low), 0)


def span_forward_tables():
    cos_tw, sin_tw = wave(np.arange(8), np.arange(128), 1024)
    twiddle = np.concatenate((cos_tw, sin_tw), 0).astype(np.float32)
    cos_t, sin_t = wave(np.arange(64), np.arange(128), 128)
    return twiddle, stacked_split(np.concatenate((cos_t, sin_t), 1))


def middle_tables():
    base = np.arange(32)
    cos32, sin32 = wave(base, base, 32)
    eye8 = np.eye(8)
    over_px = stacked_split(np.concatenate((np.kron(cos32, eye8), np.kron(-sin32, eye8)), 0))
    cos_tw, sin_tw = wave(base, base, 1024)
    spread = lambda t: np.repeat(np.tile(t, (1, 4)), 8, 0)
    front_twiddle = np.concatenate((spread(cos_tw), spread(sin_tw)), 0).astype(np.float32)
    eye2 = np.eye(2)
    block = lambda t: np.kron(eye2, t)
    within = stacked_split(np.block([[block(cos32), block(sin32)], [block(-sin32), block(cos32)]]))
    back = np.zeros((8, 2, 2, 4, 2, 2, 32))
    for py in range(8):
        for i in range(4):
            c, s = cos32[4 * py + i], sin32[4 * py + i]
            for s2 in range(2):
                back[py, 0, s2, i, s2, 0] = c
                back[py, 0, s2, i, s2, 1] = -s
                back[py, 1, s2, i, s2, 0] = s
                back[py, 1, s2, i, s2, 1] = c
    back = stacked_split(back.reshape(128, 128))
    first = np.zeros((8, 2, 4, 2, 2, 32))
    second = np.zeros((8, 2, 4, 2, 2, 32))
    for py in range(8):
        for i in range(4):
            c, s = cos_tw[4 * py + i], sin_tw[4 * py + i]
            first[py, :, i, 0] = c
            first[py, :, i, 1] = -s
            second[py, :, i, 0] = s
            second[py, :, i, 1] = c
    back_twiddle = np.concatenate((first.reshape(64, 128), second.reshape(64, 128)), 0).astype(np.float32)
    final = stacked_split(np.concatenate((np.kron(eye2, cos32), np.kron(eye2, sin32)), 1))
    return over_px, front_twiddle, within, back, back_twiddle, final


def span_inverse_tables():
    cos_t, sin_t = wave(np.arange(64), np.arange(128), 128)
    one = 2.0 * np.concatenate((cos_t, sin_t), 1)
    table = stacked_split(np.kron(np.eye(2), one))
    cos_tw, sin_tw = wave(np.arange(8), np.arange(128), 1024)
    return table, np.concatenate((cos_tw, sin_tw), 0).astype(np.float32)


def split(x):
    high = x.astype(BF16)
    return high, (x - high.astype(F32)).astype(BF16)


def dot_nn(a, b):
    return lax.dot_general(a, b, (((1,), (0,)), ((), ())), preferred_element_type=F32)


def dot_nt(a, b):
    return lax.dot_general(a, b, (((1,), (1,)), ((), ())), preferred_element_type=F32)


def table_times(dot, table, high, low):
    rows = table.shape[0] // 2
    both = dot(table, high)
    return both[:rows] + both[rows:] + dot(table[:rows], low)


def span_forward_kernel(v_ref, twiddle_ref, table_ref, out_ref):
    x = [v_ref[pl.ds(s, 96, stride=8), :] for s in range(8)]
    e = [x[s] + x[s + 4] for s in range(4)]
    o = [x[s] - x[s + 4] for s in range(4)]
    e02, e13 = e[0] + e[2], e[1] + e[3]
    om, op = ROOT_HALF * (o[1] - o[3]), ROOT_HALF * (o[1] + o[3])
    e02m, e13m = e[0] - e[2], e[1] - e[3]
    one = (o[0] + om, -(o[2] + op))
    three = (o[0] - om, o[2] - op)
    spec = [
        (e02 + e13, None),
        one,
        (e02m, -e13m),
        three,
        (e02 - e13, None),
        (three[0], -three[1]),
        (e02m, e13m),
        (one[0], -one[1]),
    ]
    parts = []
    for k1 in range(8):
        re, im = spec[k1]
        c = twiddle_ref[pl.ds(k1, 1), :]
        s = twiddle_ref[pl.ds(8 + k1, 1), :]
        if k1 == 0:
            new_re, new_im = re, jnp.zeros_like(re)
        elif im is None:
            new_re, new_im = re * c, -(re * s)
        else:
            new_re, new_im = re * c + im * s, im * c - re * s
        parts.append((split(new_re), split(new_im)))
    table = table_ref[...]
    for j in range(4):
        columns = []
        for level in range(2):
            rows = []
            for c in range(3):
                cut = slice(32 * c, 32 * c + 32)
                for turn in range(2):
                    for k1 in (2 * j, 2 * j + 1):
                        re, im = parts[k1][0][level][cut], parts[k1][1][level][cut]
                        rows.append(jnp.concatenate((re, im) if turn == 0 else (im, -re), 1))
            columns.append(jnp.concatenate(rows, 0))
        result = table_times(dot_nt, table, columns[0], columns[1])
        for c in range(3):
            out_ref[pl.ds(192 * j + c, 64, stride=3), :] = result[:, 128 * c : 128 * c + 128]


def middle_kernel(anchor, band_ref, r_ref, over_px_ref, front_tw_ref, within_ref, back_ref, back_tw_ref, final_ref, out_ref):
    data = jnp.concatenate([r_ref[pl.ds(c, 256, stride=3), :] for c in range(3)], 1)
    high, low = split(data)
    turned = table_times(dot_nn, over_px_ref[...], high, low)
    cos_tw, sin_tw = front_tw_ref[:256, :], front_tw_ref[256:, :]
    lane = lax.broadcasted_iota(jnp.int32, (1, 128), 1)
    sign = jnp.where(lane < 64, -1.0, 1.0).astype(F32)
    spectrum = []
    for c in range(3):
        p, q = turned[:256, 128 * c : 128 * c + 128], turned[256:, 128 * c : 128 * c + 128]
        a = p * cos_tw + q * sin_tw
        b = q * cos_tw - p * sin_tw
        u_high, u_low = split(a + pltpu.roll(b, 64, axis=1) * sign)
        out = table_times(dot_nt, within_ref[...], u_high, u_low)
        spectrum.append((out[:64], out[64:]))
    sub = lax.broadcasted_iota(jnp.int32, (8, 128), 0)
    lanes = lax.broadcasted_iota(jnp.int32, (8, 128), 1)
    band = jnp.zeros((8, 128), jnp.int32)
    count_one = jnp.int32(0)
    for y in range(8):
        band = jnp.where(sub == y, band_ref[y], band)
        count_one = count_one + band_ref[y]
    lane_band = (lanes // 32) % 2
    in_band = band == lane_band
    select = jnp.concatenate(
        [jnp.where(jnp.logical_and(in_band, lanes % 32 == k1), 1.0, 0.0).astype(F32) for k1 in range(32)], 0
    ).astype(BF16)
    one_f = jnp.full((8, 128), count_one, jnp.int32).astype(F32)
    count = jnp.where(lane_band == 1, one_f, 8.0 - one_f)
    weight = 1.0 / (count * float(NX * NZ * 1024))
    row64 = lax.broadcasted_iota(jnp.int32, (64, 128), 0)
    lane64 = lax.broadcasted_iota(jnp.int32, (64, 128), 1)
    scale = jnp.concatenate([weight] * 8, 0)
    scale = jnp.where(jnp.logical_and(anchor, row64 < 32), 0.5 * scale, scale)
    mean = jnp.logical_and(anchor, jnp.logical_and(row64 == 0, lane64 % 32 == 0))
    scale = jnp.where(mean, 0.0, scale)
    banded = []
    for left, right in PAIR_LIST:
        lr, li = spectrum[left]
        rr, ri = spectrum[right]
        values = [lr * rr + li * ri]
        if left != right:
            values.append(lr * ri - li * rr)
        sums = []
        for value in values:
            value_high, value_low = split(value)
            sums.append((dot_nn(value_high, select) + dot_nn(value_low, select)) * scale)
        if left == right:
            sums.append(jnp.zeros((64, 128), F32))
        banded.append(sums)
    columns = []
    for k in range(2):
        for sp in range(3):
            cut = slice(32 * k, 32 * k + 32)
            columns.append(jnp.concatenate([banded[2 * sp + s2][part][cut] for s2 in range(2) for part in range(2)], 0))
    x_high, x_low = split(jnp.concatenate(columns, 1))
    v = table_times(dot_nn, back_ref[...], x_high, x_low)
    pad = jnp.zeros((32, 128), F32)
    for py in range(8):
        t1 = back_tw_ref[pl.ds(8 * py, 8), :]
        t2 = back_tw_ref[pl.ds(64 + 8 * py, 8), :]
        re_rows, im_rows = [], []
        for column in range(6):
            cut = slice(128 * column, 128 * column + 128)
            vr, vi = v[16 * py : 16 * py + 8, cut], v[16 * py + 8 : 16 * py + 16, cut]
            re_rows.append(vr * t1 - vi * t2)
            im_rows.append(vr * t2 + vi * t1)
        rows_high, rows_low = split(jnp.concatenate(re_rows + im_rows + [pad], 0))
        out = table_times(dot_nt, final_ref[...], rows_high, rows_low)
        for b in range(2):
            out_ref[pl.ds(2 * py + b, 32, stride=16), :] = out[32 * b : 32 * b + 32]


def span_inverse_kernel(r_ref, table_ref, twiddle_ref, out_ref):
    table = table_ref[...]
    lhs = []
    for b in range(2):
        rows = r_ref[pl.ds(b, 256, stride=2), :].T
        for jp in range(2):
            lhs.append(rows[:96, 128 * jp : 128 * jp + 128])
    high, low = split(jnp.concatenate(lhs, 0))
    sums = dot_nn(high, table[:128]) + dot_nn(high, table[128:]) + dot_nn(low, table[:128])
    sub = lax.broadcasted_iota(jnp.int32, (8, 128), 0)
    for b in range(2):
        for sp in range(3):
            y = []
            for k1 in range(8):
                j, k = k1 // 2, k1 % 2
                row = (b * 2 + j // 2) * 96 + k * 24 + sp * 8
                col = (j % 2) * 256
                rc, rs = sums[row : row + 8, col : col + 128], sums[row : row + 8, col + 128 : col + 256]
                ic, is_ = sums[row + 48 : row + 56, col : col + 128], sums[row + 48 : row + 56, col + 128 : col + 256]
                zr, zi = rc - is_, rs + ic
                c, s = twiddle_ref[pl.ds(k1, 1), :], twiddle_ref[pl.ds(8 + k1, 1), :]
                if k1 == 0:
                    y.append((zr, None))
                elif k1 == 4:
                    y.append((zr * c - zi * s, None))
                else:
                    y.append((zr * c - zi * s, zr * s + zi * c))
            a = [None] + [y[k][0] + y[8 - k][0] for k in (1, 2, 3)]
            d = [None] + [y[k][1] - y[8 - k][1] for k in (1, 2, 3)]
            up, um = y[0][0] + y[4][0], y[0][0] - y[4][0]
            ap, am = a[1] + a[3], ROOT_HALF * (a[1] - a[3])
            dm, dp = d[1] - d[3], ROOT_HALF * (d[1] + d[3])
            upp, upm = up + a[2], up - a[2]
            ump, umm = um + d[2], um - d[2]
            outs = [
                upp + ap,
                umm + am - dp,
                upm - dm,
                ump - am - dp,
                upp - ap,
                umm - am + dp,
                upm + dm,
                ump + am + dp,
            ]
            for half in range(4):
                v0, v1 = outs[2 * half], outs[2 * half + 1]
                base = (sp * 2 * 2 + b) * 32 + half * 8
                out_ref[pl.ds(base, 8), :] = jnp.where(sub < 4, v0, pltpu.roll(v1, 4, axis=0))
                out_ref[pl.ds(base + 64, 8), :] = jnp.where(sub < 4, pltpu.roll(v0, 4, axis=0), v1)


def vmem(count):
    return [pl.BlockSpec(memory_space=pltpu.VMEM)] * count


def call(kernel, out_shape, in_specs, name):
    return pl.pallas_call(
        kernel,
        out_shape=jax.ShapeDtypeStruct(out_shape, F32),
        in_specs=in_specs,
        out_specs=pl.BlockSpec(memory_space=pltpu.VMEM),
        name=name,
    )


def run_span_forward(velocity):
    twiddle, table = span_forward_tables()
    return call(span_forward_kernel, (768, 128), vmem(3), "span_forward")(velocity, twiddle, table)


def run_middle(received, band_of, anchor=None):
    def kernel(band_ref, *refs):
        if anchor is None:
            at_anchor = jnp.logical_and(lax.axis_index("px") == 0, lax.axis_index("py") == 0)
        else:
            at_anchor = anchor
        middle_kernel(at_anchor, band_ref, *refs)

    specs = [pl.BlockSpec(memory_space=pltpu.SMEM)] + vmem(7)
    return call(kernel, (512, 128), specs, "middle")(band_of, received, *middle_tables())


def run_span_inverse(received):
    return call(span_inverse_kernel, (384, 128), vmem(3), "span_inverse")(received, *span_inverse_tables())


def per_device(velocity, band_of):
    sent = run_span_forward(velocity.reshape(768, 128))
    received = lax.all_to_all(sent.reshape(256, 1, 384), ("px", "py"), 0, 0, tiled=True)
    back = run_middle(received.reshape(768, 128), band_of)
    gathered = lax.all_to_all(back.reshape(256, 1, 256), ("px", "py"), 0, 0, tiled=True)
    out = run_span_inverse(gathered.reshape(512, 128))
    return out.reshape(6, 2, 8, 4, 128).transpose(0, 1, 3, 2, 4).reshape(6, 2, 4, 1024)


def solution(mesh):
    in_specs = (P(None, "px", "py", None), P())
    out_specs = P(None, None, ("px", "py"), None)
    return jax.shard_map(per_device, mesh=mesh, in_specs=in_specs, out_specs=out_specs, check_vma=False)
```

profile of v0, /device:TPU:1, one launch (start us, length us, event | category | flops | bytes accessed | tf_op | source)
XLA Modules:
  0.0 65.4 jit_solution(4394912109291268802)
XLA Ops:
  0.0 2.4 %span_forward.1 = f32[768,128]{1,0:T(8,128)} custom-call(f32[768,128]{1,0:T(8,128)} %bitcast.14, f32[16,128]{1,0:T(8,128)} %constant.18.clone.twiddle_ref, bf16[128,256]{1,0:T(8,128)(2,1)} %constant.19.clone.table_ref), custom_call_target="tpu_custom_call" | custom-call | tf_op jit(solution)/shard_map/span_forward/pallas_call | solution.py:289
  2.4 34.2 %all_to_all.10 = f32[256,1,384]{2,1,0:T(1,128)} all-to-all(f32[256,1,384]{2,1,0:T(1,128)} %bitcast.11), channel_id=1, replica_groups=mesh['px'=32,'py'=8] {'px','py'}, dimensions={0} | all-to-all | bytes 786432 | tf_op jit(solution)/shard_map/all_to_all | solution.py:310
  36.6 3.9 %middle.1 = f32[512,128]{1,0:T(8,128)} custom-call(s32[8]{0:T(128)} %band_ref.1, f32[768,128]{1,0:T(8,128)} %bitcast.10, bf16[1024,256]{1,0:T(8,128)(2,1)} %constant.20.clone.refs_1_, f32[512,128]{1,0:T(8,128)} %constant.21.clone.refs_2_, bf16[256,128]{1,0:T(8,128)(2,1)} %constant.22.clone.refs_3_, bf16[256,128]{1,0:T(8,128)(2,1)} %constant.23.clone.refs_4_, ...), custom_call_target="tpu_custom_call" | custom-call | tf_op jit(solution)/shard_map/middle/pallas_call | solution.py:301
  40.5 22.7 %all_to_all.11 = f32[256,1,256]{2,1,0:T(1,128)} all-to-all(f32[256,1,256]{2,1,0:T(1,128)} %bitcast.12), channel_id=1, replica_groups=mesh['px'=32,'py'=8] {'px','py'}, dimensions={0} | all-to-all | bytes 524288 | tf_op jit(solution)/shard_map/all_to_all | solution.py:312
  63.2 2.2 %span_inverse.1 = f32[384,128]{1,0:T(8,128)} custom-call(f32[512,128]{1,0:T(8,128)} %bitcast.13, bf16[256,512]{1,0:T(8,128)(2,1)} %constant.26.clone.table_ref, f32[16,128]{1,0:T(8,128)} %constant.18.clone.twiddle_ref), custom_call_target="tpu_custom_call" | custom-call | tf_op jit(solution)/shard_map/span_inverse/pallas_call | solution.py:305
where the time goes:
time: 65.6 us; the launch traced here: 65.4 us
  blocking collectives  56.9 us (87%)
  Pallas kernels  8.54 us (13%)
    all_to_all x1, blocking collectives, per_device(): lax.all_to_all(sent.reshape(256, 1, 384), ('px', 'py'), 0, 0, tiled=True)  34.2 us
    all_to_all x1, blocking collectives, per_device(): lax.all_to_all(back.reshape(256, 1, 256), ('px', 'py'), 0, 0, tiled=True)  22.7 us
    pallas_call x1, Pallas kernels, run_middle(): call(kernel, (512, 128), specs, 'middle')  3.9 us
    pallas_call x1, Pallas kernels, run_span_forward(): call(span_forward_kernel, (768, 128), vmem(3), 'span_forward')  2.39 us
    pallas_call x1, Pallas kernels, run_span_inverse(): call(span_inverse_kernel, (384, 128), vmem(3), 'span_inverse')  2.25 us

commit v1 on v0

--- a/solution.py
+++ b/solution.py
@@ -281,6 +281,7 @@
         in_specs=in_specs,
         out_specs=pl.BlockSpec(memory_space=pltpu.VMEM),
         name=name,
+        compiler_params=pltpu.CompilerParams(vmem_limit_bytes=16 * 1024 * 1024),
     )
 
 

time: 65.6 us -> 63.1 us (0.962)
  Pallas kernels: 8.54 us -> 4.33 us
  local copies, waits for them, and re-layouts: 0 us -> 3.18 us
  blocking collectives: 56.9 us -> 55.2 us
    unnamed x0 -> x22, local copies, waits for them, and re-layouts: none -> 3.18 us
    pallas_call x1, Pallas kernels: 2.39 us -> 0.63 us  [run_span_forward(): call(span_forward_kernel, (768, 128), vmem(3), 'span_forward')]
    all_to_all x1, blocking collectives: 22.7 us -> 21.3 us  [per_device(): lax.all_to_all(back.reshape(256, 1, 256), ('px', 'py'), 0, 0, tiled=True)]
    pallas_call x1, Pallas kernels: 3.9 us -> 2.48 us  [run_middle(): call(kernel, (512, 128), specs, 'middle')]
    pallas_call x1, Pallas kernels: 2.25 us -> 1.22 us  [run_span_inverse(): call(span_inverse_kernel, (384, 128), vmem(3), 'span_inverse')]
where the time goes in v1:
time: 63.1 us; the launch traced here: 62.8 us
  blocking collectives  55.2 us (87%)
  Pallas kernels  4.33 us (7%)
  local copies, waits for them, and re-layouts  3.18 us (5%)
    all_to_all x1, blocking collectives, per_device(): lax.all_to_all(sent.reshape(256, 1, 384), ('px', 'py'), 0, 0, tiled=True)  33.9 us
    all_to_all x1, blocking collectives, per_device(): lax.all_to_all(back.reshape(256, 1, 256), ('px', 'py'), 0, 0, tiled=True)  21.3 us
    unnamed x22, local copies, waits for them, and re-layouts  3.18 us
    pallas_call x1, Pallas kernels, run_middle(): call(kernel, (512, 128), specs, 'middle')  2.48 us

profile of v1, /device:TPU:1, one launch (start us, length us, event | category | flops | bytes accessed | tf_op | source)
XLA Modules:
  0.0 62.8 jit_solution(16955536093202976488)
XLA Ops:
  0.0 0.0 copy-start.8
  0.0 0.7 %copy-done.8 = f32[16,128]{1,0:T(8,128)S(1)} copy-done((f32[16,128]{1,0:T(8,128)S(1)}, f32[16,128]{1,0:T(8,128)}, u32[]{:S(2)}) %copy-start.8) | copy-done | bytes 8216
  0.7 0.0 copy-start.1
  0.7 1.0 %copy-done.1 = f32[3,32,1,1024]{3,2,1,0:T(1,128)S(1)} copy-done((f32[3,32,1,1024]{3,2,1,0:T(1,128)S(1)}, f32[3,32,1,1024]{3,2,1,0:T(1,128)}, u32[]{:S(2)}) %copy-start.1) | copy-done | bytes 393240
  1.7 0.0 copy-start.7
  1.7 0.8 %copy-done.7 = bf16[128,256]{1,0:T(8,128)(2,1)S(1)} copy-done((bf16[128,256]{1,0:T(8,128)(2,1)S(1)}, bf16[128,256]{1,0:T(8,128)(2,1)}, u32[]{:S(2)}) %copy-start.7) | copy-done | bytes 65560
  2.5 0.0 copy-start.4
  2.5 0.0 copy-start.5
  2.5 0.0 copy-start.6
  2.5 0.0 copy-start.9
  2.5 0.6 span_forward.1
  3.2 0.0 copy-start
  3.2 0.0 copy-start.3
  3.2 33.9 %all_to_all.10 = f32[256,1,384]{2,1,0:T(1,128)S(1)} all-to-all(f32[256,1,384]{2,1,0:T(1,128)S(1)} %bitcast.11), channel_id=1, replica_groups=mesh['px'=32,'py'=8] {'px','py'}, dimensions={0} | all-to-all | bytes 786432 | tf_op jit(solution)/shard_map/all_to_all | solution.py:311
  37.1 0.0 copy-start.10
  37.1 0.0 copy-done.4
  37.1 0.0 copy-done.5
  37.1 0.0 copy-done.6
  37.1 0.0 copy-done.9
  37.1 0.0 copy-done
  37.2 0.0 copy-done.3
  37.2 0.6 copy-done.10
  37.8 2.5 %middle.1 = f32[512,128]{1,0:T(8,128)S(1)} custom-call(s32[8]{0:T(128)S(1)} %copy-done.10, f32[768,128]{1,0:T(8,128)S(1)} %bitcast.10, bf16[1024,256]{1,0:T(8,128)(2,1)S(1)} %copy-done, f32[512,128]{1,0:T(8,128)S(1)} %copy-done.3, bf16[256,128]{1,0:T(8,128)(2,1)S(1)} %copy-done.6, bf16[256,128]{1,0:T(8,128)(2,1)S(1)} %copy-done.5, f32[128,128]{1,0:T(8,128)S(1)} %copy-done.4, ...), custom_call_target="tpu_custom_call" | custom-call | tf_op jit(solution)/shard_map/middle/pallas_call | solution.py:302
  40.3 0.0 copy-start.2
  40.3 21.3 %all_to_all.11 = f32[256,1,256]{2,1,0:T(1,128)S(1)} all-to-all(f32[256,1,256]{2,1,0:T(1,128)S(1)} %bitcast.12), channel_id=1, replica_groups=mesh['px'=32,'py'=8] {'px','py'}, dimensions={0} | all-to-all | bytes 524288 | tf_op jit(solution)/shard_map/all_to_all | solution.py:313
  61.6 0.0 copy-done.2
  61.6 1.2 %span_inverse.1 = f32[384,128]{1,0:T(8,128)} custom-call(f32[512,128]{1,0:T(8,128)S(1)} %bitcast.13, bf16[256,512]{1,0:T(8,128)(2,1)S(1)} %copy-done.2, f32[16,128]{1,0:T(8,128)S(1)} %copy-done.8), custom_call_target="tpu_custom_call" | custom-call | tf_op jit(solution)/shard_map/span_inverse/pallas_call | solution.py:306
Async XLA Ops:
  0.0 0.7 %copy-start.8 = (f32[16,128]{1,0:T(8,128)S(1)}, f32[16,128]{1,0:T(8,128)}, u32[]{:S(2)}) copy-start(f32[16,128]{1,0:T(8,128)} %constant.18.clone.twiddle_ref) | copy-start | bytes 24580
  0.7 1.0 %copy-start.1 = (f32[3,32,1,1024]{3,2,1,0:T(1,128)S(1)}, f32[3,32,1,1024]{3,2,1,0:T(1,128)}, u32[]{:S(2)}) copy-start(f32[3,32,1,1024]{3,2,1,0:T(1,128)} %param.12) | copy-start | bytes 1179652
  1.7 0.8 %copy-start.7 = (bf16[128,256]{1,0:T(8,128)(2,1)S(1)}, bf16[128,256]{1,0:T(8,128)(2,1)}, u32[]{:S(2)}) copy-start(bf16[128,256]{1,0:T(8,128)(2,1)} %constant.19.clone.table_ref) | copy-start | bytes 196612
  2.5 34.6 %copy-start.4 = (f32[128,128]{1,0:T(8,128)S(1)}, f32[128,128]{1,0:T(8,128)}, u32[]{:S(2)}) copy-start(f32[128,128]{1,0:T(8,128)} %constant.24.clone.refs_5_) | copy-start | bytes 196612
  2.5 34.6 %copy-start.5 = (bf16[256,128]{1,0:T(8,128)(2,1)S(1)}, bf16[256,128]{1,0:T(8,128)(2,1)}, u32[]{:S(2)}) copy-start(bf16[256,128]{1,0:T(8,128)(2,1)} %constant.23.clone.refs_4_) | copy-start | bytes 196612
  2.5 34.6 %copy-start.6 = (bf16[256,128]{1,0:T(8,128)(2,1)S(1)}, bf16[256,128]{1,0:T(8,128)(2,1)}, u32[]{:S(2)}) copy-start(bf16[256,128]{1,0:T(8,128)(2,1)} %constant.22.clone.refs_3_) | copy-start | bytes 196612
  2.5 34.6 %copy-start.9 = (bf16[128,128]{1,0:T(8,128)(2,1)S(1)}, bf16[128,128]{1,0:T(8,128)(2,1)}, u32[]{:S(2)}) copy-start(bf16[128,128]{1,0:T(8,128)(2,1)} %constant.25.clone.refs_6_) | copy-start | bytes 98308
  3.2 34.0 %copy-start = (bf16[1024,256]{1,0:T(8,128)(2,1)S(1)}, bf16[1024,256]{1,0:T(8,128)(2,1)}, u32[]{:S(2)}) copy-start(bf16[1024,256]{1,0:T(8,128)(2,1)} %constant.20.clone.refs_1_) | copy-start | bytes 1572868
  3.2 34.0 %copy-start.3 = (f32[512,128]{1,0:T(8,128)S(1)}, f32[512,128]{1,0:T(8,128)}, u32[]{:S(2)}) copy-start(f32[512,128]{1,0:T(8,128)} %constant.21.clone.refs_2_) | copy-start | bytes 786436
  37.1 0.7 %copy-start.10 = (s32[8]{0:T(128)S(1)}, s32[8]{0:T(128)}, u32[]{:S(2)}) copy-start(s32[8]{0:T(128)} %band_ref.1) | copy-start | bytes 100
  40.3 21.3 %copy-start.2 = (bf16[256,512]{1,0:T(8,128)(2,1)S(1)}, bf16[256,512]{1,0:T(8,128)(2,1)}, u32[]{:S(2)}) copy-start(bf16[256,512]{1,0:T(8,128)(2,1)} %constant.26.clone.table_ref) | copy-start | bytes 786436

commit v2 on v1

--- a/solution.py
+++ b/solution.py
@@ -98,55 +98,68 @@
     return both[:rows] + both[rows:] + dot(table[:rows], low)
 
 
-def span_forward_kernel(v_ref, twiddle_ref, table_ref, out_ref):
-    x = [v_ref[pl.ds(s, 96, stride=8), :] for s in range(8)]
-    e = [x[s] + x[s + 4] for s in range(4)]
-    o = [x[s] - x[s + 4] for s in range(4)]
-    e02, e13 = e[0] + e[2], e[1] + e[3]
-    om, op = ROOT_HALF * (o[1] - o[3]), ROOT_HALF * (o[1] + o[3])
-    e02m, e13m = e[0] - e[2], e[1] - e[3]
-    one = (o[0] + om, -(o[2] + op))
-    three = (o[0] - om, o[2] - op)
-    spec = [
-        (e02 + e13, None),
-        one,
-        (e02m, -e13m),
-        three,
-        (e02 - e13, None),
-        (three[0], -three[1]),
-        (e02m, e13m),
-        (one[0], -one[1]),
+def span_forward_kernel(v_hbm, twiddle_hbm, table_hbm, out_ref, v_ref, twiddle_ref, table_ref, sems):
+    copies = [
+        pltpu.make_async_copy(v_hbm.at[pl.ds(256 * c, 256)], v_ref.at[pl.ds(256 * c, 256)], sems.at[c]) for c in range(3)
     ]
-    parts = []
-    for k1 in range(8):
-        re, im = spec[k1]
-        c = twiddle_ref[pl.ds(k1, 1), :]
-        s = twiddle_ref[pl.ds(8 + k1, 1), :]
-        if k1 == 0:
-            new_re, new_im = re, jnp.zeros_like(re)
-        elif im is None:
-            new_re, new_im = re * c, -(re * s)
-        else:
-            new_re, new_im = re * c + im * s, im * c - re * s
-        parts.append((split(new_re), split(new_im)))
-    table = table_ref[...]
-    for j in range(4):
+    copies.append(pltpu.make_async_copy(twiddle_hbm, twiddle_ref, sems.at[3]))
+    copies.append(pltpu.make_async_copy(table_hbm, table_ref, sems.at[4]))
+    for c in (3, 0, 4, 1, 2):
+        copies[c].start()
+    copies[3].wait()
+    for c in range(3):
+        copies[c].wait()
+        x = [v_ref[pl.ds(256 * c + s, 32, stride=8), :] for s in range(8)]
+        e = [x[s] + x[s + 4] for s in range(4)]
+        o = [x[s] - x[s + 4] for s in range(4)]
+        e02, e13 = e[0] + e[2], e[1] + e[3]
+        om, op = ROOT_HALF * (o[1] - o[3]), ROOT_HALF * (o[1] + o[3])
+        e02m, e13m = e[0] - e[2], e[1] - e[3]
+        one = (o[0] + om, -(o[2] + op))
+        three = (o[0] - om, o[2] - op)
+        spec = [
+            (e02 + e13, None),
+            one,
+            (e02m, -e13m),
+            three,
+            (e02 - e13, None),
+            (three[0], -three[1]),
+            (e02m, e13m),
+            (one[0], -one[1]),
+        ]
+        parts = []
+        for k1 in range(8):
+            re, im = spec[k1]
+            cos_tw = twiddle_ref[pl.ds(k1, 1), :]
+            sin_tw = twiddle_ref[pl.ds(8 + k1, 1), :]
+            if k1 == 0:
+                new_re, new_im = re, jnp.zeros_like(re)
+            elif im is None:
+                new_re, new_im = re * cos_tw, -(re * sin_tw)
+            else:
+                new_re, new_im = re * cos_tw + im * sin_tw, im * cos_tw - re * sin_tw
+            parts.append((split(new_re), split(new_im)))
         columns = []
         for level in range(2):
             rows = []
-            for c in range(3):
-                cut = slice(32 * c, 32 * c + 32)
+            for j in range(4):
                 for turn in range(2):
                     for k1 in (2 * j, 2 * j + 1):
-                        re, im = parts[k1][0][level][cut], parts[k1][1][level][cut]
+                        re, im = parts[k1][0][level], parts[k1][1][level]
                         rows.append(jnp.concatenate((re, im) if turn == 0 else (im, -re), 1))
             columns.append(jnp.concatenate(rows, 0))
-        result = table_times(dot_nt, table, columns[0], columns[1])
-        for c in range(3):
-            out_ref[pl.ds(192 * j + c, 64, stride=3), :] = result[:, 128 * c : 128 * c + 128]
-
-
-def middle_kernel(anchor, band_ref, r_ref, over_px_ref, front_tw_ref, within_ref, back_ref, back_tw_ref, final_ref, out_ref):
+        if c == 0:
+            copies[4].wait()
+        result = table_times(dot_nt, table_ref[...], columns[0], columns[1])
+        for j in range(4):
+            out_ref[pl.ds(192 * j + c, 64, stride=3), :] = result[:, 128 * j : 128 * j + 128]
+
+
+def middle_kernel(
+    anchor, band_hbm, r_ref, over_px_ref, front_tw_ref, within_ref, back_ref, back_tw_ref, final_ref, out_ref, band_ref, sem
+):
+    band_copy = pltpu.make_async_copy(band_hbm, band_ref, sem)
+    band_copy.start()
     data = jnp.concatenate([r_ref[pl.ds(c, 256, stride=3), :] for c in range(3)], 1)
     high, low = split(data)
     turned = table_times(dot_nn, over_px_ref[...], high, low)
@@ -163,6 +176,7 @@
         spectrum.append((out[:64], out[64:]))
     sub = lax.broadcasted_iota(jnp.int32, (8, 128), 0)
     lanes = lax.broadcasted_iota(jnp.int32, (8, 128), 1)
+    band_copy.wait()
     band = jnp.zeros((8, 128), jnp.int32)
     count_one = jnp.int32(0)
     for y in range(8):
@@ -219,7 +233,8 @@
             out_ref[pl.ds(2 * py + b, 32, stride=16), :] = out[32 * b : 32 * b + 32]
 
 
-def span_inverse_kernel(r_ref, table_ref, twiddle_ref, out_ref):
+def span_inverse_kernel(r_ref, table_ref, twiddle_ref, out_hbm, out_ref, sems):
+    copies = []
     table = table_ref[...]
     lhs = []
     for b in range(2):
@@ -229,8 +244,8 @@
     high, low = split(jnp.concatenate(lhs, 0))
     sums = dot_nn(high, table[:128]) + dot_nn(high, table[128:]) + dot_nn(low, table[:128])
     sub = lax.broadcasted_iota(jnp.int32, (8, 128), 0)
-    for b in range(2):
-        for sp in range(3):
+    for sp in range(3):
+        for b in range(2):
             y = []
             for k1 in range(8):
                 j, k = k1 // 2, k1 % 2
@@ -268,42 +283,60 @@
                 base = (sp * 2 * 2 + b) * 32 + half * 8
                 out_ref[pl.ds(base, 8), :] = jnp.where(sub < 4, v0, pltpu.roll(v1, 4, axis=0))
                 out_ref[pl.ds(base + 64, 8), :] = jnp.where(sub < 4, pltpu.roll(v0, 4, axis=0), v1)
-
-
-def vmem(count):
-    return [pl.BlockSpec(memory_space=pltpu.VMEM)] * count
-
-
-def call(kernel, out_shape, in_specs, name):
+        block = pl.ds(128 * sp, 128)
+        copies.append(pltpu.make_async_copy(out_ref.at[block], out_hbm.at[block], sems.at[sp]))
+        copies[-1].start()
+    for copy in copies:
+        copy.wait()
+
+
+def spaces(*kinds):
+    return [pl.BlockSpec(memory_space=kind) for kind in kinds]
+
+
+VMEM, HBM = pltpu.VMEM, pltpu.HBM
+
+
+def call(kernel, out_shape, in_specs, name, out_space=VMEM, scratch=()):
     return pl.pallas_call(
         kernel,
         out_shape=jax.ShapeDtypeStruct(out_shape, F32),
         in_specs=in_specs,
-        out_specs=pl.BlockSpec(memory_space=pltpu.VMEM),
+        out_specs=pl.BlockSpec(memory_space=out_space),
+        scratch_shapes=list(scratch),
         name=name,
         compiler_params=pltpu.CompilerParams(vmem_limit_bytes=16 * 1024 * 1024),
     )
 
 
+def in_hbm(x):
+    return pltpu.with_memory_space_constraint(jnp.asarray(x), HBM)
+
+
 def run_span_forward(velocity):
     twiddle, table = span_forward_tables()
-    return call(span_forward_kernel, (768, 128), vmem(3), "span_forward")(velocity, twiddle, table)
+    scratch = (VMEM((768, 128), F32), VMEM(twiddle.shape, F32), VMEM(table.shape, BF16), pltpu.SemaphoreType.DMA((5,)))
+    run = call(span_forward_kernel, (768, 128), spaces(HBM, HBM, HBM), "span_forward", scratch=scratch)
+    return run(in_hbm(velocity), in_hbm(twiddle), in_hbm(table))
 
 
 def run_middle(received, band_of, anchor=None):
-    def kernel(band_ref, *refs):
+    def kernel(*refs):
         if anchor is None:
             at_anchor = jnp.logical_and(lax.axis_index("px") == 0, lax.axis_index("py") == 0)
         else:
             at_anchor = anchor
-        middle_kernel(at_anchor, band_ref, *refs)
-
-    specs = [pl.BlockSpec(memory_space=pltpu.SMEM)] + vmem(7)
-    return call(kernel, (512, 128), specs, "middle")(band_of, received, *middle_tables())
+        middle_kernel(at_anchor, *refs)
+
+    scratch = (pltpu.SMEM((8,), jnp.int32), pltpu.SemaphoreType.DMA)
+    run = call(kernel, (512, 128), spaces(HBM, *[VMEM] * 7), "middle", scratch=scratch)
+    return run(in_hbm(band_of), received, *middle_tables())
 
 
 def run_span_inverse(received):
-    return call(span_inverse_kernel, (384, 128), vmem(3), "span_inverse")(received, *span_inverse_tables())
+    scratch = (VMEM((384, 128), F32), pltpu.SemaphoreType.DMA((3,)))
+    run = call(span_inverse_kernel, (384, 128), spaces(VMEM, VMEM, VMEM), "span_inverse", HBM, scratch)
+    return run(received, *span_inverse_tables())
 
 
 def per_device(velocity, band_of):

time: 63.1 us -> 60.8 us (0.964)
  local copies, waits for them, and re-layouts: 3.18 us -> 0.05 us
  Pallas kernels: 4.33 us -> 5.27 us
    unnamed x22 -> x16, local copies, waits for them, and re-layouts: 3.18 us -> 0.05 us
    pallas_call x3, Pallas kernels: 4.33 us -> 5.27 us  [the longest x1 2.06 us: run_middle(): return run(in_hbm(band_of), received, *middle_tables())]
where the time goes in v2:
time: 60.8 us; the launch traced here: 60.6 us
  blocking collectives  55.2 us (91%)
  Pallas kernels  5.27 us (9%)
    all_to_all x1, blocking collectives, per_device(): lax.all_to_all(sent.reshape(256, 1, 384), ('px', 'py'), 0, 0, tiled=True)  33.9 us
    all_to_all x1, blocking collectives, per_device(): lax.all_to_all(back.reshape(256, 1, 256), ('px', 'py'), 0, 0, tiled=True)  21.3 us
    pallas_call x1, Pallas kernels, run_middle(): return run(in_hbm(band_of), received, *middle_tables())  2.06 us
    pallas_call x1, Pallas kernels, run_span_forward(): return run(in_hbm(velocity), in_hbm(twiddle), in_hbm(table))  1.99 us
    pallas_call x1, Pallas kernels, run_span_inverse(): return run(received, *span_inverse_tables())  1.22 us

profile of v2, /device:TPU:1, one launch (start us, length us, event | category | flops | bytes accessed | tf_op | source)
XLA Modules:
  0.0 60.6 jit_solution(965147691633219889)
XLA Ops:
  0.0 0.0 copy-start.3
  0.0 0.0 copy-start.4
  0.0 0.0 copy-start.5
  0.0 0.0 copy-start.7
  0.0 2.0 %span_forward.1 = f32[768,128]{1,0:T(8,128)S(1)} custom-call(f32[768,128]{1,0:T(8,128)} %bitcast.14, f32[16,128]{1,0:T(8,128)} %constant.18.clone.twiddle_hbm.twiddle_ref, bf16[128,256]{1,0:T(8,128)(2,1)} %constant.19.clone.table_hbm), custom_call_target="tpu_custom_call" | custom-call | tf_op jit(solution)/shard_map/span_forward/pallas_call | solution.py:320
  2.0 0.0 copy-start
  2.0 0.0 copy-start.2
  2.0 33.9 %all_to_all.10 = f32[256,1,384]{2,1,0:T(1,128)S(1)} all-to-all(f32[256,1,384]{2,1,0:T(1,128)S(1)} %bitcast.11), channel_id=1, replica_groups=mesh['px'=32,'py'=8] {'px','py'}, dimensions={0} | all-to-all | bytes 786432 | tf_op jit(solution)/shard_map/all_to_all | solution.py:344
  36.0 0.0 copy-done.3
  36.0 0.0 copy-done.4
  36.0 0.0 copy-done.5
  36.0 0.0 copy-done.7
  36.0 0.0 copy-done
  36.0 0.0 copy-done.2
  36.0 2.1 %middle.1 = f32[512,128]{1,0:T(8,128)S(1)} custom-call(s32[8]{0:T(128)} %refs_0_.1, f32[768,128]{1,0:T(8,128)S(1)} %bitcast.10, bf16[1024,256]{1,0:T(8,128)(2,1)S(1)} %copy-done, f32[512,128]{1,0:T(8,128)S(1)} %copy-done.2, bf16[256,128]{1,0:T(8,128)(2,1)S(1)} %copy-done.5, bf16[256,128]{1,0:T(8,128)(2,1)S(1)} %copy-done.4, f32[128,128]{1,0:T(8,128)S(1)} %copy-done.3, ...), custom_call_target="tpu_custom_call" | custom-call | tf_op jit(solution)/shard_map/middle/pallas_call | solution.py:333
  38.1 0.0 copy-start.1
  38.1 0.0 copy-start.6
  38.1 21.3 %all_to_all.11 = f32[256,1,256]{2,1,0:T(1,128)S(1)} all-to-all(f32[256,1,256]{2,1,0:T(1,128)S(1)} %bitcast.12), channel_id=1, replica_groups=mesh['px'=32,'py'=8] {'px','py'}, dimensions={0} | all-to-all | bytes 524288 | tf_op jit(solution)/shard_map/all_to_all | solution.py:346
  59.4 0.0 copy-done.1
  59.4 0.0 copy-done.6
  59.4 1.2 %span_inverse.1 = f32[384,128]{1,0:T(8,128)} custom-call(f32[512,128]{1,0:T(8,128)S(1)} %bitcast.13, bf16[256,512]{1,0:T(8,128)(2,1)S(1)} %copy-done.1, f32[16,128]{1,0:T(8,128)S(1)} %copy-done.6), custom_call_target="tpu_custom_call" | custom-call | tf_op jit(solution)/shard_map/span_inverse/pallas_call | solution.py:339
Async XLA Ops:
  0.0 36.0 %copy-start.3 = (f32[128,128]{1,0:T(8,128)S(1)}, f32[128,128]{1,0:T(8,128)}, u32[]{:S(2)}) copy-start(f32[128,128]{1,0:T(8,128)} %constant.24.clone.refs_6_) | copy-start | bytes 196612
  0.0 36.0 %copy-start.4 = (bf16[256,128]{1,0:T(8,128)(2,1)S(1)}, bf16[256,128]{1,0:T(8,128)(2,1)}, u32[]{:S(2)}) copy-start(bf16[256,128]{1,0:T(8,128)(2,1)} %constant.23.clone.refs_5_) | copy-start | bytes 196612
  0.0 36.0 %copy-start.5 = (bf16[256,128]{1,0:T(8,128)(2,1)S(1)}, bf16[256,128]{1,0:T(8,128)(2,1)}, u32[]{:S(2)}) copy-start(bf16[256,128]{1,0:T(8,128)(2,1)} %constant.22.clone.refs_4_) | copy-start | bytes 196612
  0.0 36.0 %copy-start.7 = (bf16[128,128]{1,0:T(8,128)(2,1)S(1)}, bf16[128,128]{1,0:T(8,128)(2,1)}, u32[]{:S(2)}) copy-start(bf16[128,128]{1,0:T(8,128)(2,1)} %constant.25.clone.refs_7_) | copy-start | bytes 98308
  2.0 34.0 %copy-start = (bf16[1024,256]{1,0:T(8,128)(2,1)S(1)}, bf16[1024,256]{1,0:T(8,128)(2,1)}, u32[]{:S(2)}) copy-start(bf16[1024,256]{1,0:T(8,128)(2,1)} %constant.20.clone.refs_2_) | copy-start | bytes 1572868
  2.0 34.0 %copy-start.2 = (f32[512,128]{1,0:T(8,128)S(1)}, f32[512,128]{1,0:T(8,128)}, u32[]{:S(2)}) copy-start(f32[512,128]{1,0:T(8,128)} %constant.21.clone.refs_3_) | copy-start | bytes 786436
  38.1 21.3 %copy-start.1 = (bf16[256,512]{1,0:T(8,128)(2,1)S(1)}, bf16[256,512]{1,0:T(8,128)(2,1)}, u32[]{:S(2)}) copy-start(bf16[256,512]{1,0:T(8,128)(2,1)} %constant.26.clone.table_ref) | copy-start | bytes 786436
  38.1 21.3 %copy-start.6 = (f32[16,128]{1,0:T(8,128)S(1)}, f32[16,128]{1,0:T(8,128)}, u32[]{:S(2)}) copy-start(f32[16,128]{1,0:T(8,128)} %constant.18.clone.twiddle_hbm.twiddle_ref) | copy-start | bytes 24580

commit v3 on v1

--- a/solution.py
+++ b/solution.py
@@ -23,30 +23,47 @@
     return np.cos(angle), np.sin(angle)
 
 
-def stacked_split(table):
+def three_part(table, axis=1):
     high = table.astype(np.float32).astype(jnp.bfloat16)
     low = (table - high.astype(np.float64)).astype(np.float32).astype(jnp.bfloat16)
-    return np.concatenate((high, low), 0)
+    return np.concatenate((high, high, low), axis)
+
+
+def paired(table):
+    parts = three_part(table)
+    width = table.shape[1]
+    return np.concatenate((parts[:, : 2 * width], np.concatenate((parts[:, 2 * width :], 0 * parts[:, :width]), 1)), 0)
 
 
 def span_forward_tables():
     cos_tw, sin_tw = wave(np.arange(8), np.arange(128), 1024)
     twiddle = np.concatenate((cos_tw, sin_tw), 0).astype(np.float32)
     cos_t, sin_t = wave(np.arange(64), np.arange(128), 128)
-    return twiddle, stacked_split(np.concatenate((cos_t, sin_t), 1))
+    parts = three_part(np.concatenate((cos_t, sin_t), 1))
+    return twiddle, np.concatenate((parts[:, :256], parts[:, 512:]), 0)
 
 
 def middle_tables():
     base = np.arange(32)
     cos32, sin32 = wave(base, base, 32)
     eye8 = np.eye(8)
-    over_px = stacked_split(np.concatenate((np.kron(cos32, eye8), np.kron(-sin32, eye8)), 0))
+    over_px = three_part(np.concatenate((np.kron(cos32[:17], eye8), np.kron(-sin32[1:16], eye8)), 0))
     cos_tw, sin_tw = wave(base, base, 1024)
     spread = lambda t: np.repeat(np.tile(t, (1, 4)), 8, 0)
-    front_twiddle = np.concatenate((spread(cos_tw), spread(sin_tw)), 0).astype(np.float32)
+    turn_sign = np.where(base < 16, 1.0, -1.0)[:, None]
+    lane_sign = np.where(np.arange(128) < 64, 1.0, -1.0)
+    front_twiddle = np.concatenate(
+        (
+            spread(cos_tw),
+            spread(turn_sign * sin_tw),
+            spread(turn_sign * cos_tw) * lane_sign,
+            -spread(sin_tw) * lane_sign,
+        ),
+        0,
+    ).astype(np.float32)
     eye2 = np.eye(2)
     block = lambda t: np.kron(eye2, t)
-    within = stacked_split(np.block([[block(cos32), block(sin32)], [block(-sin32), block(cos32)]]))
+    within = paired(np.block([[block(cos32), block(sin32)], [block(-sin32), block(cos32)]]))
     back = np.zeros((8, 2, 2, 4, 2, 2, 32))
     for py in range(8):
         for i in range(4):
@@ -56,7 +73,7 @@
                 back[py, 0, s2, i, s2, 1] = -s
                 back[py, 1, s2, i, s2, 0] = s
                 back[py, 1, s2, i, s2, 1] = c
-    back = stacked_split(back.reshape(128, 128))
+    back = paired(back.reshape(128, 128))
     first = np.zeros((8, 2, 4, 2, 2, 32))
     second = np.zeros((8, 2, 4, 2, 2, 32))
     for py in range(8):
@@ -67,14 +84,14 @@
             second[py, :, i, 0] = s
             second[py, :, i, 1] = c
     back_twiddle = np.concatenate((first.reshape(64, 128), second.reshape(64, 128)), 0).astype(np.float32)
-    final = stacked_split(np.concatenate((np.kron(eye2, cos32), np.kron(eye2, sin32)), 1))
+    final = paired(np.concatenate((np.kron(eye2, cos32), np.kron(eye2, sin32)), 1))
     return over_px, front_twiddle, within, back, back_twiddle, final
 
 
 def span_inverse_tables():
     cos_t, sin_t = wave(np.arange(64), np.arange(128), 128)
     one = 2.0 * np.concatenate((cos_t, sin_t), 1)
-    table = stacked_split(np.kron(np.eye(2), one))
+    table = three_part(np.kron(np.eye(2), one), 0)
     cos_tw, sin_tw = wave(np.arange(8), np.arange(128), 1024)
     return table, np.concatenate((cos_tw, sin_tw), 0).astype(np.float32)
 
@@ -84,6 +101,16 @@
     return high, (x - high.astype(F32)).astype(BF16)
 
 
+def joined(x, axis):
+    high, low = split(x)
+    return jnp.concatenate((high, low, high), axis)
+
+
+def halves_added(x):
+    rows = x.shape[0] // 2
+    return x[:rows] + x[rows:]
+
+
 def dot_nn(a, b):
     return lax.dot_general(a, b, (((1,), (0,)), ((), ())), preferred_element_type=F32)
 
@@ -92,13 +119,16 @@
     return lax.dot_general(a, b, (((1,), (1,)), ((), ())), preferred_element_type=F32)
 
 
-def table_times(dot, table, high, low):
-    rows = table.shape[0] // 2
-    both = dot(table, high)
-    return both[:rows] + both[rows:] + dot(table[:rows], low)
-
-
-def span_forward_kernel(v_ref, twiddle_ref, table_ref, out_ref):
+def span_forward_kernel(v_hbm, twiddle_hbm, table_hbm, out_ref, v_ref, twiddle_ref, table_ref, sems):
+    copies = [
+        pltpu.make_async_copy(v_hbm, v_ref, sems.at[0]),
+        pltpu.make_async_copy(twiddle_hbm, twiddle_ref, sems.at[1]),
+        pltpu.make_async_copy(table_hbm, table_ref, sems.at[2]),
+    ]
+    for copy in copies:
+        copy.start()
+    for copy in copies:
+        copy.wait()
     x = [v_ref[pl.ds(s, 96, stride=8), :] for s in range(8)]
     e = [x[s] + x[s + 4] for s in range(4)]
     o = [x[s] - x[s + 4] for s in range(4)]
@@ -120,14 +150,14 @@
     parts = []
     for k1 in range(8):
         re, im = spec[k1]
-        c = twiddle_ref[pl.ds(k1, 1), :]
-        s = twiddle_ref[pl.ds(8 + k1, 1), :]
+        cos_tw = twiddle_ref[pl.ds(k1, 1), :]
+        sin_tw = twiddle_ref[pl.ds(8 + k1, 1), :]
         if k1 == 0:
             new_re, new_im = re, jnp.zeros_like(re)
         elif im is None:
-            new_re, new_im = re * c, -(re * s)
+            new_re, new_im = re * cos_tw, -(re * sin_tw)
         else:
-            new_re, new_im = re * c + im * s, im * c - re * s
+            new_re, new_im = re * cos_tw + im * sin_tw, im * cos_tw - re * sin_tw
         parts.append((split(new_re), split(new_im)))
     table = table_ref[...]
     for j in range(4):
@@ -141,28 +171,37 @@
                         re, im = parts[k1][0][level][cut], parts[k1][1][level][cut]
                         rows.append(jnp.concatenate((re, im) if turn == 0 else (im, -re), 1))
             columns.append(jnp.concatenate(rows, 0))
-        result = table_times(dot_nt, table, columns[0], columns[1])
+        result = halves_added(dot_nt(table, columns[0])) + dot_nt(table[:64], columns[1])
         for c in range(3):
             out_ref[pl.ds(192 * j + c, 64, stride=3), :] = result[:, 128 * c : 128 * c + 128]
 
 
-def middle_kernel(anchor, band_ref, r_ref, over_px_ref, front_tw_ref, within_ref, back_ref, back_tw_ref, final_ref, out_ref):
+def middle_kernel(
+    anchor, band_hbm, r_ref, over_px_ref, front_tw_ref, within_ref, back_ref, back_tw_ref, final_ref, out_ref, band_ref, sem
+):
+    band_copy = pltpu.make_async_copy(band_hbm, band_ref, sem)
+    band_copy.start()
     data = jnp.concatenate([r_ref[pl.ds(c, 256, stride=3), :] for c in range(3)], 1)
-    high, low = split(data)
-    turned = table_times(dot_nn, over_px_ref[...], high, low)
-    cos_tw, sin_tw = front_tw_ref[:256, :], front_tw_ref[256:, :]
-    lane = lax.broadcasted_iota(jnp.int32, (1, 128), 1)
-    sign = jnp.where(lane < 64, -1.0, 1.0).astype(F32)
+    turned = dot_nn(over_px_ref[...], joined(data, 0))
     spectrum = []
     for c in range(3):
-        p, q = turned[:256, 128 * c : 128 * c + 128], turned[256:, 128 * c : 128 * c + 128]
-        a = p * cos_tw + q * sin_tw
-        b = q * cos_tw - p * sin_tw
-        u_high, u_low = split(a + pltpu.roll(b, 64, axis=1) * sign)
-        out = table_times(dot_nt, within_ref[...], u_high, u_low)
+        cut = slice(128 * c, 128 * c + 128)
+        rows = []
+        for k1 in range(32):
+            t1, t2, t3, t4 = [front_tw_ref[pl.ds(256 * t + 8 * k1, 8), :] for t in range(4)]
+            m = min(k1, 32 - k1)
+            p = turned[8 * m : 8 * m + 8, cut]
+            if m % 16 == 0:
+                rows.append(p * t1 + pltpu.roll(p * t4, 64, axis=1))
+            else:
+                q = turned[128 + 8 * m : 136 + 8 * m, cut]
+                rows.append((p * t1 + q * t2) + pltpu.roll(q * t3 + p * t4, 64, axis=1))
+        u = jnp.concatenate(split(jnp.concatenate(rows, 0)), 1)
+        out = halves_added(dot_nt(within_ref[...], u))
         spectrum.append((out[:64], out[64:]))
     sub = lax.broadcasted_iota(jnp.int32, (8, 128), 0)
     lanes = lax.broadcasted_iota(jnp.int32, (8, 128), 1)
+    band_copy.wait()
     band = jnp.zeros((8, 128), jnp.int32)
     count_one = jnp.int32(0)
     for y in range(8):
@@ -173,6 +212,7 @@
     select = jnp.concatenate(
         [jnp.where(jnp.logical_and(in_band, lanes % 32 == k1), 1.0, 0.0).astype(F32) for k1 in range(32)], 0
     ).astype(BF16)
+    select = jnp.concatenate((select, select), 0)
     one_f = jnp.full((8, 128), count_one, jnp.int32).astype(F32)
     count = jnp.where(lane_band == 1, one_f, 8.0 - one_f)
     weight = 1.0 / (count * float(NX * NZ * 1024))
@@ -191,8 +231,7 @@
             values.append(lr * ri - li * rr)
         sums = []
         for value in values:
-            value_high, value_low = split(value)
-            sums.append((dot_nn(value_high, select) + dot_nn(value_low, select)) * scale)
+            sums.append(dot_nn(jnp.concatenate(split(value), 1), select) * scale)
         if left == right:
             sums.append(jnp.zeros((64, 128), F32))
         banded.append(sums)
@@ -201,8 +240,11 @@
         for sp in range(3):
             cut = slice(32 * k, 32 * k + 32)
             columns.append(jnp.concatenate([banded[2 * sp + s2][part][cut] for s2 in range(2) for part in range(2)], 0))
-    x_high, x_low = split(jnp.concatenate(columns, 1))
-    v = table_times(dot_nn, back_ref[...], x_high, x_low)
+    v = halves_added(dot_nn(back_ref[...], jnp.concatenate(split(jnp.concatenate(columns, 1)), 0)))
+    middle_tail(v, back_tw_ref, final_ref, out_ref)
+
+
+def middle_tail(v, back_tw_ref, final_ref, out_ref):
     pad = jnp.zeros((32, 128), F32)
     for py in range(8):
         t1 = back_tw_ref[pl.ds(8 * py, 8), :]
@@ -213,24 +255,23 @@
             vr, vi = v[16 * py : 16 * py + 8, cut], v[16 * py + 8 : 16 * py + 16, cut]
             re_rows.append(vr * t1 - vi * t2)
             im_rows.append(vr * t2 + vi * t1)
-        rows_high, rows_low = split(jnp.concatenate(re_rows + im_rows + [pad], 0))
-        out = table_times(dot_nt, final_ref[...], rows_high, rows_low)
+        out = halves_added(dot_nt(final_ref[...], jnp.concatenate(split(jnp.concatenate(re_rows + im_rows + [pad], 0)), 1)))
         for b in range(2):
             out_ref[pl.ds(2 * py + b, 32, stride=16), :] = out[32 * b : 32 * b + 32]
 
 
-def span_inverse_kernel(r_ref, table_ref, twiddle_ref, out_ref):
+def span_inverse_kernel(r_ref, table_ref, twiddle_ref, out_hbm, out_ref, sems):
+    copies = []
     table = table_ref[...]
     lhs = []
     for b in range(2):
         rows = r_ref[pl.ds(b, 256, stride=2), :].T
         for jp in range(2):
             lhs.append(rows[:96, 128 * jp : 128 * jp + 128])
-    high, low = split(jnp.concatenate(lhs, 0))
-    sums = dot_nn(high, table[:128]) + dot_nn(high, table[128:]) + dot_nn(low, table[:128])
+    sums = dot_nn(joined(jnp.concatenate(lhs, 0), 1), table)
     sub = lax.broadcasted_iota(jnp.int32, (8, 128), 0)
-    for b in range(2):
-        for sp in range(3):
+    for sp in range(3):
+        for b in range(2):
             y = []
             for k1 in range(8):
                 j, k = k1 // 2, k1 % 2
@@ -268,42 +309,60 @@
                 base = (sp * 2 * 2 + b) * 32 + half * 8
                 out_ref[pl.ds(base, 8), :] = jnp.where(sub < 4, v0, pltpu.roll(v1, 4, axis=0))
                 out_ref[pl.ds(base + 64, 8), :] = jnp.where(sub < 4, pltpu.roll(v0, 4, axis=0), v1)
-
-
-def vmem(count):
-    return [pl.BlockSpec(memory_space=pltpu.VMEM)] * count
-
-
-def call(kernel, out_shape, in_specs, name):
+        block = pl.ds(128 * sp, 128)
+        copies.append(pltpu.make_async_copy(out_ref.at[block], out_hbm.at[block], sems.at[sp]))
+        copies[-1].start()
+    for copy in copies:
+        copy.wait()
+
+
+def spaces(*kinds):
+    return [pl.BlockSpec(memory_space=kind) for kind in kinds]
+
+
+VMEM, HBM = pltpu.VMEM, pltpu.HBM
+
+
+def call(kernel, out_shape, in_specs, name, out_space=VMEM, scratch=()):
     return pl.pallas_call(
         kernel,
         out_shape=jax.ShapeDtypeStruct(out_shape, F32),
         in_specs=in_specs,
-        out_specs=pl.BlockSpec(memory_space=pltpu.VMEM),
+        out_specs=pl.BlockSpec(memory_space=out_space),
+        scratch_shapes=list(scratch),
         name=name,
         compiler_params=pltpu.CompilerParams(vmem_limit_bytes=16 * 1024 * 1024),
     )
 
 
+def in_hbm(x):
+    return pltpu.with_memory_space_constraint(jnp.asarray(x), HBM)
+
+
 def run_span_forward(velocity):
     twiddle, table = span_forward_tables()
-    return call(span_forward_kernel, (768, 128), vmem(3), "span_forward")(velocity, twiddle, table)
+    scratch = (VMEM((768, 128), F32), VMEM(twiddle.shape, F32), VMEM(table.shape, BF16), pltpu.SemaphoreType.DMA((3,)))
+    run = call(span_forward_kernel, (768, 128), spaces(HBM, HBM, HBM), "span_forward", scratch=scratch)
+    return run(in_hbm(velocity), in_hbm(twiddle), in_hbm(table))
 
 
 def run_middle(received, band_of, anchor=None):
-    def kernel(band_ref, *refs):
+    def kernel(*refs):
         if anchor is None:
             at_anchor = jnp.logical_and(lax.axis_index("px") == 0, lax.axis_index("py") == 0)
         else:
             at_anchor = anchor
-        middle_kernel(at_anchor, band_ref, *refs)
-
-    specs = [pl.BlockSpec(memory_space=pltpu.SMEM)] + vmem(7)
-    return call(kernel, (512, 128), specs, "middle")(band_of, received, *middle_tables())
+        middle_kernel(at_anchor, *refs)
+
+    scratch = (pltpu.SMEM((8,), jnp.int32), pltpu.SemaphoreType.DMA)
+    run = call(kernel, (512, 128), spaces(HBM, *[VMEM] * 7), "middle", scratch=scratch)
+    return run(in_hbm(band_of), received, *middle_tables())
 
 
 def run_span_inverse(received):
-    return call(span_inverse_kernel, (384, 128), vmem(3), "span_inverse")(received, *span_inverse_tables())
+    scratch = (VMEM((384, 128), F32), pltpu.SemaphoreType.DMA((3,)))
+    run = call(span_inverse_kernel, (384, 128), spaces(VMEM, VMEM, VMEM), "span_inverse", HBM, scratch)
+    return run(received, *span_inverse_tables())
 
 
 def per_device(velocity, band_of):

time: 63.1 us -> 60 us (0.951)
  local copies, waits for them, and re-layouts: 3.18 us -> 0.05 us
    unnamed x22 -> x16, local copies, waits for them, and re-layouts: 3.18 us -> 0.05 us
where the time goes in v3:
time: 60 us; the launch traced here: 59.8 us
  blocking collectives  55.2 us (92%)
  Pallas kernels  4.47 us (7%)
    all_to_all x1, blocking collectives, per_device(): lax.all_to_all(sent.reshape(256, 1, 384), ('px', 'py'), 0, 0, tiled=True)  33.9 us
    all_to_all x1, blocking collectives, per_device(): lax.all_to_all(back.reshape(256, 1, 256), ('px', 'py'), 0, 0, tiled=True)  21.3 us
    pallas_call x1, Pallas kernels, run_span_forward(): return run(in_hbm(velocity), in_hbm(twiddle), in_hbm(table))  1.72 us
    pallas_call x1, Pallas kernels, run_middle(): return run(in_hbm(band_of), received, *middle_tables())  1.63 us

profile of v3, /device:TPU:1, one launch (start us, length us, event | category | flops | bytes accessed | tf_op | source)
XLA Modules:
  0.0 59.8 jit_solution(10699095740437468028)
XLA Ops:
  0.0 0.0 copy-start.2
  0.0 0.0 copy-start.5
  0.0 0.0 copy-start.6
  0.0 1.7 %span_forward.1 = f32[768,128]{1,0:T(8,128)S(1)} custom-call(f32[768,128]{1,0:T(8,128)} %bitcast.14, f32[16,128]{1,0:T(8,128)} %constant.18.clone.twiddle_hbm.twiddle_ref, bf16[128,256]{1,0:T(8,128)(2,1)} %constant.19.clone.table_hbm), custom_call_target="tpu_custom_call" | custom-call | tf_op jit(solution)/shard_map/span_forward/pallas_call | solution.py:346
  1.7 0.0 copy-start
  1.7 0.0 copy-start.3
  1.8 0.0 copy-start.4
  1.8 33.9 %all_to_all.10 = f32[256,1,384]{2,1,0:T(1,128)S(1)} all-to-all(f32[256,1,384]{2,1,0:T(1,128)S(1)} %bitcast.11), channel_id=1, replica_groups=mesh['px'=32,'py'=8] {'px','py'}, dimensions={0} | all-to-all | bytes 786432 | tf_op jit(solution)/shard_map/all_to_all | solution.py:370
  35.7 0.0 copy-done.2
  35.7 0.0 copy-done.5
  35.7 0.0 copy-done.6
  35.7 0.0 copy-done
  35.7 0.0 copy-done.3
  35.7 0.0 copy-done.4
  35.7 1.6 %middle.1 = f32[512,128]{1,0:T(8,128)S(1)} custom-call(s32[8]{0:T(128)} %refs_0_.1, f32[768,128]{1,0:T(8,128)S(1)} %bitcast.10, bf16[256,768]{1,0:T(8,128)(2,1)S(1)} %copy-done.2, f32[1024,128]{1,0:T(8,128)S(1)} %copy-done, bf16[256,256]{1,0:T(8,128)(2,1)S(1)} %copy-done.4, bf16[256,256]{1,0:T(8,128)(2,1)S(1)} %copy-done.3, f32[128,128]{1,0:T(8,128)S(1)} %copy-done.6, ...), custom_call_target="tpu_custom_call" | custom-call | tf_op jit(solution)/shard_map/middle/pallas_call | solution.py:359
  37.4 0.0 copy-start.1
  37.4 0.0 copy-start.7
  37.4 21.3 %all_to_all.11 = f32[256,1,256]{2,1,0:T(1,128)S(1)} all-to-all(f32[256,1,256]{2,1,0:T(1,128)S(1)} %bitcast.12), channel_id=1, replica_groups=mesh['px'=32,'py'=8] {'px','py'}, dimensions={0} | all-to-all | bytes 524288 | tf_op jit(solution)/shard_map/all_to_all | solution.py:372
  58.7 0.0 copy-done.1
  58.7 0.0 copy-done.7
  58.7 1.1 %span_inverse.1 = f32[384,128]{1,0:T(8,128)} custom-call(f32[512,128]{1,0:T(8,128)S(1)} %bitcast.13, bf16[384,512]{1,0:T(8,128)(2,1)S(1)} %copy-done.1, f32[16,128]{1,0:T(8,128)S(1)} %copy-done.7), custom_call_target="tpu_custom_call" | custom-call | tf_op jit(solution)/shard_map/span_inverse/pallas_call | solution.py:365
Async XLA Ops:
  0.0 35.7 %copy-start.2 = (bf16[256,768]{1,0:T(8,128)(2,1)S(1)}, bf16[256,768]{1,0:T(8,128)(2,1)}, u32[]{:S(2)}) copy-start(bf16[256,768]{1,0:T(8,128)(2,1)} %constant.20.clone.refs_2_) | copy-start | bytes 1179652
  0.0 35.7 %copy-start.5 = (bf16[128,256]{1,0:T(8,128)(2,1)S(1)}, bf16[128,256]{1,0:T(8,128)(2,1)}, u32[]{:S(2)}) copy-start(bf16[128,256]{1,0:T(8,128)(2,1)} %constant.25.clone.refs_7_) | copy-start | bytes 196612
  0.0 35.7 %copy-start.6 = (f32[128,128]{1,0:T(8,128)S(1)}, f32[128,128]{1,0:T(8,128)}, u32[]{:S(2)}) copy-start(f32[128,128]{1,0:T(8,128)} %constant.24.clone.refs_6_) | copy-start | bytes 196612
  1.7 34.0 %copy-start = (f32[1024,128]{1,0:T(8,128)S(1)}, f32[1024,128]{1,0:T(8,128)}, u32[]{:S(2)}) copy-start(f32[1024,128]{1,0:T(8,128)} %constant.21.clone.refs_3_) | copy-start | bytes 1572868
  1.7 34.0 %copy-start.3 = (bf16[256,256]{1,0:T(8,128)(2,1)S(1)}, bf16[256,256]{1,0:T(8,128)(2,1)}, u32[]{:S(2)}) copy-start(bf16[256,256]{1,0:T(8,128)(2,1)} %constant.23.clone.refs_5_) | copy-start | bytes 393220
  1.8 34.0 %copy-start.4 = (bf16[256,256]{1,0:T(8,128)(2,1)S(1)}, bf16[256,256]{1,0:T(8,128)(2,1)}, u32[]{:S(2)}) copy-start(bf16[256,256]{1,0:T(8,128)(2,1)} %constant.22.clone.refs_4_) | copy-start | bytes 393220
  37.4 21.3 %copy-start.1 = (bf16[384,512]{1,0:T(8,128)(2,1)S(1)}, bf16[384,512]{1,0:T(8,128)(2,1)}, u32[]{:S(2)}) copy-start(bf16[384,512]{1,0:T(8,128)(2,1)} %constant.26.clone.table_ref) | copy-start | bytes 1179652
  37.4 21.3 %copy-start.7 = (f32[16,128]{1,0:T(8,128)S(1)}, f32[16,128]{1,0:T(8,128)}, u32[]{:S(2)}) copy-start(f32[16,128]{1,0:T(8,128)} %constant.18.clone.twiddle_hbm.twiddle_ref) | copy-start | bytes 24580

commit v4 on v3

--- a/solution.py
+++ b/solution.py
@@ -74,18 +74,18 @@
                 back[py, 1, s2, i, s2, 0] = s
                 back[py, 1, s2, i, s2, 1] = c
     back = paired(back.reshape(128, 128))
-    first = np.zeros((8, 2, 4, 2, 2, 32))
-    second = np.zeros((8, 2, 4, 2, 2, 32))
-    for py in range(8):
-        for i in range(4):
-            c, s = cos_tw[4 * py + i], sin_tw[4 * py + i]
-            first[py, :, i, 0] = c
-            first[py, :, i, 1] = -s
-            second[py, :, i, 0] = s
-            second[py, :, i, 1] = c
-    back_twiddle = np.concatenate((first.reshape(64, 128), second.reshape(64, 128)), 0).astype(np.float32)
-    final = paired(np.concatenate((np.kron(eye2, cos32), np.kron(eye2, sin32)), 1))
-    return over_px, front_twiddle, within, back, back_twiddle, final
+    back_twiddle = np.zeros((2, 2, 8, 2, 4, 2, 2, 32))
+    for core in range(2):
+        c, s = wave(32 * core + base, base, 1024)
+        c, s = (t.reshape(8, 1, 4, 1, 32) for t in (c, s))
+        back_twiddle[core, 0, :, :, :, 0] = c
+        back_twiddle[core, 0, :, :, :, 1] = -s
+        back_twiddle[core, 1, :, :, :, 0] = s
+        back_twiddle[core, 1, :, :, :, 1] = c
+    back_twiddle = back_twiddle.reshape(256, 128).astype(np.float32)
+    cos16, sin16 = wave(np.arange(16), base, 16)
+    final = paired(np.concatenate((np.kron(eye2, cos16), np.kron(eye2, sin16)), 1))
+    return (over_px, front_twiddle, within), (back, back_twiddle, final)
 
 
 def span_inverse_tables():
@@ -173,12 +173,12 @@
             columns.append(jnp.concatenate(rows, 0))
         result = halves_added(dot_nt(table, columns[0])) + dot_nt(table[:64], columns[1])
         for c in range(3):
-            out_ref[pl.ds(192 * j + c, 64, stride=3), :] = result[:, 128 * c : 128 * c + 128]
-
-
-def middle_kernel(
-    anchor, band_hbm, r_ref, over_px_ref, front_tw_ref, within_ref, back_ref, back_tw_ref, final_ref, out_ref, band_ref, sem
-):
+            for t in range(8):
+                first = 384 * (j // 2) + 24 * (j % 2) + 48 * t + c
+                out_ref[pl.ds(first, 8, stride=3), :] = result[8 * t : 8 * t + 8, 128 * c : 128 * c + 128]
+
+
+def middle_front_kernel(anchor, band_hbm, r_ref, over_px_ref, front_tw_ref, within_ref, out_ref, band_ref, sem):
     band_copy = pltpu.make_async_copy(band_hbm, band_ref, sem)
     band_copy.start()
     data = jnp.concatenate([r_ref[pl.ds(c, 256, stride=3), :] for c in range(3)], 1)
@@ -222,63 +222,70 @@
     scale = jnp.where(jnp.logical_and(anchor, row64 < 32), 0.5 * scale, scale)
     mean = jnp.logical_and(anchor, jnp.logical_and(row64 == 0, lane64 % 32 == 0))
     scale = jnp.where(mean, 0.0, scale)
-    banded = []
+    place = 0
     for left, right in PAIR_LIST:
         lr, li = spectrum[left]
         rr, ri = spectrum[right]
         values = [lr * rr + li * ri]
         if left != right:
             values.append(lr * ri - li * rr)
-        sums = []
         for value in values:
-            sums.append(dot_nn(jnp.concatenate(split(value), 1), select) * scale)
-        if left == right:
-            sums.append(jnp.zeros((64, 128), F32))
-        banded.append(sums)
+            out_ref[64 * place : 64 * place + 64, :] = dot_nn(jnp.concatenate(split(value), 1), select) * scale
+            place += 1
+
+
+def middle_back_kernel(core, own_ref, got_ref, back_ref, back_tw_ref, final_ref, out_ref):
+    first_core = core == 0
+    zeros = jnp.zeros((32, 128), F32)
     columns = []
-    for k in range(2):
-        for sp in range(3):
-            cut = slice(32 * k, 32 * k + 32)
-            columns.append(jnp.concatenate([banded[2 * sp + s2][part][cut] for s2 in range(2) for part in range(2)], 0))
+    for g in range(2):
+        for k in range(2):
+            place, pieces = 0, []
+            for left, right in PAIR_LIST:
+                for part in range(2):
+                    if part == 1 and left == right:
+                        pieces.append(zeros)
+                        continue
+                    rows = slice(64 * place + 32 * k, 64 * place + 32 * k + 32)
+                    own, got = own_ref[rows, :], got_ref[rows, :]
+                    pieces.append(jnp.where(first_core, own, got) if g == 0 else jnp.where(first_core, got, own))
+                    place += 1
+            for sp in range(3):
+                columns.append(jnp.concatenate(pieces[4 * sp : 4 * sp + 4], 0))
     v = halves_added(dot_nn(back_ref[...], jnp.concatenate(split(jnp.concatenate(columns, 1)), 0)))
-    middle_tail(v, back_tw_ref, final_ref, out_ref)
-
-
-def middle_tail(v, back_tw_ref, final_ref, out_ref):
-    pad = jnp.zeros((32, 128), F32)
+    lane = lax.broadcasted_iota(jnp.int32, (16, 128), 1)
+    twiddle_row = pl.multiple_of(core * 128, 128)
     for py in range(8):
-        t1 = back_tw_ref[pl.ds(8 * py, 8), :]
-        t2 = back_tw_ref[pl.ds(64 + 8 * py, 8), :]
+        t1 = back_tw_ref[pl.ds(twiddle_row + 8 * py, 8), :]
+        t2 = back_tw_ref[pl.ds(twiddle_row + 64 + 8 * py, 8), :]
         re_rows, im_rows = [], []
-        for column in range(6):
+        for column in range(12):
             cut = slice(128 * column, 128 * column + 128)
             vr, vi = v[16 * py : 16 * py + 8, cut], v[16 * py + 8 : 16 * py + 16, cut]
             re_rows.append(vr * t1 - vi * t2)
             im_rows.append(vr * t2 + vi * t1)
-        out = halves_added(dot_nt(final_ref[...], jnp.concatenate(split(jnp.concatenate(re_rows + im_rows + [pad], 0)), 1)))
-        for b in range(2):
-            out_ref[pl.ds(2 * py + b, 32, stride=16), :] = out[32 * b : 32 * b + 32]
+        rows = jnp.concatenate(split(jnp.concatenate(re_rows + im_rows, 0)), 1)
+        out = halves_added(dot_nt(final_ref[...], jnp.concatenate((rows, rows[128:]), 0)))
+        out_ref[pl.ds(3 * py, 16, stride=24), :] = out[:16, :128]
+        out_ref[pl.ds(3 * py + 1, 16, stride=24), :] = jnp.where(lane < 64, out[:16, 128:], out[16:, 128:])
+        out_ref[pl.ds(3 * py + 2, 16, stride=24), :] = out[16:, :128]
 
 
 def span_inverse_kernel(r_ref, table_ref, twiddle_ref, out_hbm, out_ref, sems):
     copies = []
     table = table_ref[...]
-    lhs = []
-    for b in range(2):
-        rows = r_ref[pl.ds(b, 256, stride=2), :].T
-        for jp in range(2):
-            lhs.append(rows[:96, 128 * jp : 128 * jp + 128])
+    lhs = [r_ref[pl.ds(part, 128, stride=3), :].T for part in range(3)]
     sums = dot_nn(joined(jnp.concatenate(lhs, 0), 1), table)
     sub = lax.broadcasted_iota(jnp.int32, (8, 128), 0)
     for sp in range(3):
         for b in range(2):
             y = []
             for k1 in range(8):
-                j, k = k1 // 2, k1 % 2
-                row = (b * 2 + j // 2) * 96 + k * 24 + sp * 8
-                col = (j % 2) * 256
-                rc, rs = sums[row : row + 8, col : col + 128], sums[row : row + 8, col + 128 : col + 256]
-                ic, is_ = sums[row + 48 : row + 56, col : col + 128], sums[row + 48 : row + 56, col + 128 : col + 256]
+                col = (k1 // 4) * 256
+                at = (k1 % 4) * 24 + sp * 8
+                row_re, row_im = [n if b == 0 else (n + 256 if n < 128 else n + 64) for n in (at, at + 96)]
+                rc, rs = sums[row_re : row_re + 8, col : col + 128], sums[row_re : row_re + 8, col + 128 : col + 256]
+                ic, is_ = sums[row_im : row_im + 8, col : col + 128], sums[row_im : row_im + 8, col + 128 : col + 256]
                 zr, zi = rc - is_, rs + ic
                 c, s = twiddle_ref[pl.ds(k1, 1), :], twiddle_ref[pl.ds(8 + k1, 1), :]
                 if k1 == 0:
@@ -346,17 +353,23 @@
     return run(in_hbm(velocity), in_hbm(twiddle), in_hbm(table))
 
 
-def run_middle(received, band_of, anchor=None):
+def run_middle_front(received, band_of, anchor=None):
     def kernel(*refs):
+        at_anchor = anchor
         if anchor is None:
-            at_anchor = jnp.logical_and(lax.axis_index("px") == 0, lax.axis_index("py") == 0)
-        else:
-            at_anchor = anchor
-        middle_kernel(at_anchor, *refs)
+            at_anchor = lax.axis_index("q") + lax.axis_index("core") + lax.axis_index("py") == 0
+        middle_front_kernel(at_anchor, *refs)
 
     scratch = (pltpu.SMEM((8,), jnp.int32), pltpu.SemaphoreType.DMA)
-    run = call(kernel, (512, 128), spaces(HBM, *[VMEM] * 7), "middle", scratch=scratch)
-    return run(in_hbm(band_of), received, *middle_tables())
+    run = call(kernel, (576, 128), spaces(HBM, *[VMEM] * 4), "middle_front", scratch=scratch)
+    return run(in_hbm(band_of), received, *middle_tables()[0])
+
+
+def run_middle_back(own, got, core=None):
+    def kernel(*refs):
+        middle_back_kernel(lax.axis_index("core") if core is None else core, *refs)
+
+    return call(kernel, (384, 128), spaces(*[VMEM] * 5), "middle_back")(own, got, *middle_tables()[1])
 
 
 def run_span_inverse(received):
@@ -367,14 +380,17 @@
 
 def per_device(velocity, band_of):
     sent = run_span_forward(velocity.reshape(768, 128))
-    received = lax.all_to_all(sent.reshape(256, 1, 384), ("px", "py"), 0, 0, tiled=True)
-    back = run_middle(received.reshape(768, 128), band_of)
-    gathered = lax.all_to_all(back.reshape(256, 1, 256), ("px", "py"), 0, 0, tiled=True)
-    out = run_span_inverse(gathered.reshape(512, 128))
+    received = lax.all_to_all(sent.reshape(256, 1, 384), ("q", "core", "py"), 0, 0, tiled=True)
+    own = run_middle_front(received.reshape(768, 128), band_of)
+    got = lax.ppermute(own, "core", ((0, 1), (1, 0)))
+    back = run_middle_back(own, got)
+    gathered = lax.all_to_all(back.reshape(128, 1, 384), ("q", "py"), 0, 0, tiled=True)
+    out = run_span_inverse(gathered.reshape(384, 128))
     return out.reshape(6, 2, 8, 4, 128).transpose(0, 1, 3, 2, 4).reshape(6, 2, 4, 1024)
 
 
 def solution(mesh):
-    in_specs = (P(None, "px", "py", None), P())
-    out_specs = P(None, None, ("px", "py"), None)
-    return jax.shard_map(per_device, mesh=mesh, in_specs=in_specs, out_specs=out_specs, check_vma=False)
+    split_mesh = jax.sharding.Mesh(mesh.devices.reshape(16, 2, 8), ("q", "core", "py"))
+    in_specs = (P(None, ("q", "core"), "py", None), P())
+    out_specs = P(None, None, ("q", "core", "py"), None)
+    return jax.shard_map(per_device, mesh=split_mesh, in_specs=in_specs, out_specs=out_specs, check_vma=False)

time: 60 us -> 58.3 us (0.972)
  blocking collectives: 55.2 us -> 51.2 us
  waiting for transfers between devices: 0 us -> 1.21 us
  starting transfers between devices: 0 us -> 0.74 us
    all_to_all x2, blocking collectives: 55.2 us -> 51.2 us  [the longest x1 33.9 us: per_device(): lax.all_to_all(sent.reshape(256, 1, 384), ('q', 'core', 'py'), 0, 0, tile...]
    ppermute x0 -> x1, waiting for transfers between devices: none -> 1.21 us  [per_device(): got = lax.ppermute(own, 'core', ((0, 1), (1, 0)))]
    ppermute x0 -> x1, starting transfers between devices: none -> 0.74 us  [per_device(): got = lax.ppermute(own, 'core', ((0, 1), (1, 0)))]
    pallas_call x1 -> x2, Pallas kernels: 1.63 us -> 1.97 us  [the longest x1 1.17 us: run_middle_front(): return run(in_hbm(band_of), received, *middle_tables()[0])]
  transfers between devices with their start and end apart: 0 -> 1, of which waited for: 0 -> 1; matrix products, arithmetic and copies ran while one was open for 0% -> 0% of each run, Pallas kernels for 0% -> 0%
where the time goes in v4:
time: 58.3 us; the launch traced here: 58.1 us
  blocking collectives  51.2 us (88%)
  Pallas kernels  4.8 us (8%)
  waiting for transfers between devices  1.21 us (2%)
  starting transfers between devices  0.74 us (1%)
    all_to_all x1, blocking collectives, per_device(): lax.all_to_all(sent.reshape(256, 1, 384), ('q', 'core', 'py'), 0, 0, tile...  33.9 us
    all_to_all x1, blocking collectives, per_device(): lax.all_to_all(back.reshape(128, 1, 384), ('q', 'py'), 0, 0, tiled=True)  17.3 us
    pallas_call x1, Pallas kernels, run_span_forward(): return run(in_hbm(velocity), in_hbm(twiddle), in_hbm(table))  1.7 us
    ppermute x1, waiting for transfers between devices, per_device(): got = lax.ppermute(own, 'core', ((0, 1), (1, 0)))  1.21 us
    pallas_call x1, Pallas kernels, run_middle_front(): return run(in_hbm(band_of), received, *middle_tables()[0])  1.17 us
  transfers between devices with their start and end apart: 1, of which 1 were waited for; matrix products, arithmetic and copies ran while one was open for 0% of the time, Pallas kernels for 0%

profile of v4, /device:TPU:1, one launch (start us, length us, event | category | flops | bytes accessed | tf_op | source)
XLA Modules:
  0.0 58.1 jit_solution(8323774066952124673)
XLA Ops:
  0.0 0.0 copy-start.2
  0.0 1.7 %span_forward.1 = f32[768,128]{1,0:T(8,128)S(1)} custom-call(f32[768,128]{1,0:T(8,128)} %bitcast.14, f32[16,128]{1,0:T(8,128)} %constant.18.clone.twiddle_hbm.twiddle_ref, bf16[128,256]{1,0:T(8,128)(2,1)} %constant.19.clone.table_hbm), custom_call_target="tpu_custom_call" | custom-call | tf_op jit(solution)/shard_map/span_forward/pallas_call | solution.py:353
  1.7 0.0 copy-start
  1.7 0.0 copy-start.5
  1.7 33.9 %all_to_all.10 = f32[256,1,384]{2,1,0:T(1,128)S(1)} all-to-all(f32[256,1,384]{2,1,0:T(1,128)S(1)} %bitcast.11), channel_id=1, replica_groups=mesh['q'=16,'core'=2,'py'=8] {'q','core','py'}, dimensions={0} | all-to-all | bytes 786432 | tf_op jit(solution)/shard_map/all_to_all | solution.py:383
  35.7 0.0 copy-done.2
  35.7 0.0 copy-done
  35.7 0.0 copy-done.5
  35.7 0.0 copy-start.3
  35.7 0.0 copy-start.4
  35.7 0.0 copy-start.7
  35.7 1.2 %middle_front.1.refs_0_ = f32[576,128]{1,0:T(8,128)S(1)} custom-call(s32[8]{0:T(128)} %refs_0_.1, f32[768,128]{1,0:T(8,128)S(1)} %bitcast.10, bf16[256,768]{1,0:T(8,128)(2,1)S(1)} %copy-done.2, f32[1024,128]{1,0:T(8,128)S(1)} %copy-done, bf16[256,256]{1,0:T(8,128)(2,1)S(1)} %copy-done.5), custom_call_target="tpu_custom_call" | custom-call | tf_op jit(solution)/shard_map/middle_front/pallas_call | solution.py:365
  36.9 0.7 %collective-permute-start = (f32[576,128]{1,0:T(8,128)S(1)}, f32[576,128]{1,0:T(8,128)S(1)}, u32[]{:S(2)}, u32[]{:S(2)}) collective-permute-start(f32[576,128]{1,0:T(8,128)S(1)} %middle_front.1.refs_0_), channel_id=1, source_target_pairs={{0,8},{8,0},{1,9},{9,1},{2,10},{10,2},{3,11},{11,3},{4,12},{12,4},... | collective-permute-start | bytes 884744 | tf_op jit(solution)/shard_map/ppermute | solution.py:385
  37.6 1.2 %collective-permute-done.refs_1_ = f32[576,128]{1,0:T(8,128)S(1)} collective-permute-done((f32[576,128]{1,0:T(8,128)S(1)}, f32[576,128]{1,0:T(8,128)S(1)}, u32[]{:S(2)}, u32[]{:S(2)}) %collective-permute-start) | collective-permute-done | bytes 294944 | tf_op jit(solution)/shard_map/ppermute | solution.py:385
  38.8 0.0 copy-done.3
  38.8 0.0 copy-done.4
  38.8 0.0 copy-done.7
  38.8 0.0 copy-start.6
  38.9 0.8 %middle_back.1 = f32[384,128]{1,0:T(8,128)S(1)} custom-call(f32[576,128]{1,0:T(8,128)S(1)} %middle_front.1.refs_0_, f32[576,128]{1,0:T(8,128)S(1)} %collective-permute-done.refs_1_, bf16[256,256]{1,0:T(8,128)(2,1)S(1)} %copy-done.4, f32[256,128]{1,0:T(8,128)S(1)} %copy-done.3, bf16[64,256]{1,0:T(8,128)(2,1)S(1)} %copy-done.7), custom_call_target="tpu_custom_call" | custom-call | tf_op jit(solution)/shard_map/middle_back/pallas_call | solution.py:372
  39.7 0.0 copy-start.1
  39.7 17.3 %all_to_all.11 = f32[128,1,384]{2,1,0:T(1,128)S(1)} all-to-all(f32[128,1,384]{2,1,0:T(1,128)S(1)} %bitcast.13), channel_id=1, replica_groups=mesh['q'=16,'core'=2,'py'=8] {'q','py'}, dimensions={0} | all-to-all | bytes 393216 | tf_op jit(solution)/shard_map/all_to_all | solution.py:387
  56.9 0.0 copy-done.6
  56.9 0.0 copy-done.1
  56.9 1.1 %span_inverse.1 = f32[384,128]{1,0:T(8,128)} custom-call(f32[384,128]{1,0:T(8,128)S(1)} %bitcast.12, bf16[384,512]{1,0:T(8,128)(2,1)S(1)} %copy-done.1, f32[16,128]{1,0:T(8,128)S(1)} %copy-done.6), custom_call_target="tpu_custom_call" | custom-call | tf_op jit(solution)/shard_map/span_inverse/pallas_call | solution.py:378
Async XLA Ops:
  0.0 35.7 %copy-start.2 = (bf16[256,768]{1,0:T(8,128)(2,1)S(1)}, bf16[256,768]{1,0:T(8,128)(2,1)}, u32[]{:S(2)}) copy-start(bf16[256,768]{1,0:T(8,128)(2,1)} %constant.20.clone.refs_2_) | copy-start | bytes 1179652
  1.7 34.0 %copy-start = (f32[1024,128]{1,0:T(8,128)S(1)}, f32[1024,128]{1,0:T(8,128)}, u32[]{:S(2)}) copy-start(f32[1024,128]{1,0:T(8,128)} %constant.21.clone.refs_3_) | copy-start | bytes 1572868
  1.7 33.9 %copy-start.5 = (bf16[256,256]{1,0:T(8,128)(2,1)S(1)}, bf16[256,256]{1,0:T(8,128)(2,1)}, u32[]{:S(2)}) copy-start(bf16[256,256]{1,0:T(8,128)(2,1)} %constant.22.clone.refs_4_) | copy-start | bytes 393220
  35.7 3.2 %copy-start.3 = (f32[256,128]{1,0:T(8,128)S(1)}, f32[256,128]{1,0:T(8,128)}, u32[]{:S(2)}) copy-start(f32[256,128]{1,0:T(8,128)} %constant.24.clone.refs_3_) | copy-start | bytes 393220
  35.7 3.2 %copy-start.4 = (bf16[256,256]{1,0:T(8,128)(2,1)S(1)}, bf16[256,256]{1,0:T(8,128)(2,1)}, u32[]{:S(2)}) copy-start(bf16[256,256]{1,0:T(8,128)(2,1)} %constant.23.clone.refs_2_) | copy-start | bytes 393220
  35.7 3.2 %copy-start.7 = (bf16[64,256]{1,0:T(8,128)(2,1)S(1)}, bf16[64,256]{1,0:T(8,128)(2,1)}, u32[]{:S(2)}) copy-start(bf16[64,256]{1,0:T(8,128)(2,1)} %constant.25.clone.refs_4_) | copy-start | bytes 98308
  36.9 2.0 %collective-permute-start = (f32[576,128]{1,0:T(8,128)S(1)}, f32[576,128]{1,0:T(8,128)S(1)}, u32[]{:S(2)}, u32[]{:S(2)}) collective-permute-start(f32[576,128]{1,0:T(8,128)S(1)} %middle_front.1.refs_0_), channel_id=1, source_target_pairs={{0,8},{8,0},{1,9},{9,1},{2,10},{10,2},{3,11},{11,3},{4,12},{12,4},... | collective-permute-start | bytes 884744 | tf_op jit(solution)/shard_map/ppermute | solution.py:385
  38.8 18.1 %copy-start.6 = (f32[16,128]{1,0:T(8,128)S(1)}, f32[16,128]{1,0:T(8,128)}, u32[]{:S(2)}) copy-start(f32[16,128]{1,0:T(8,128)} %constant.18.clone.twiddle_hbm.twiddle_ref) | copy-start | bytes 24580
  39.7 17.3 %copy-start.1 = (bf16[384,512]{1,0:T(8,128)(2,1)S(1)}, bf16[384,512]{1,0:T(8,128)(2,1)}, u32[]{:S(2)}) copy-start(bf16[384,512]{1,0:T(8,128)(2,1)} %constant.26.clone.table_ref) | copy-start | bytes 1179652

commit v5 on v4

--- a/solution.py
+++ b/solution.py
@@ -39,8 +39,7 @@
     cos_tw, sin_tw = wave(np.arange(8), np.arange(128), 1024)
     twiddle = np.concatenate((cos_tw, sin_tw), 0).astype(np.float32)
     cos_t, sin_t = wave(np.arange(64), np.arange(128), 128)
-    parts = three_part(np.concatenate((cos_t, sin_t), 1))
-    return twiddle, np.concatenate((parts[:, :256], parts[:, 512:]), 0)
+    return twiddle, paired(np.concatenate((cos_t, sin_t), 0))
 
 
 def middle_tables():
@@ -160,25 +159,26 @@
             new_re, new_im = re * cos_tw + im * sin_tw, im * cos_tw - re * sin_tw
         parts.append((split(new_re), split(new_im)))
     table = table_ref[...]
+    lane = lax.broadcasted_iota(jnp.int32, (1, 384), 1) % 128
+    sign = jnp.where(lane < 64, 1.0, -1.0).astype(F32)
     for j in range(4):
-        columns = []
-        for level in range(2):
-            rows = []
-            for c in range(3):
-                cut = slice(32 * c, 32 * c + 32)
-                for turn in range(2):
-                    for k1 in (2 * j, 2 * j + 1):
-                        re, im = parts[k1][0][level][cut], parts[k1][1][level][cut]
-                        rows.append(jnp.concatenate((re, im) if turn == 0 else (im, -re), 1))
-            columns.append(jnp.concatenate(rows, 0))
-        result = halves_added(dot_nt(table, columns[0])) + dot_nt(table[:64], columns[1])
+        rows = []
+        for c in range(3):
+            cut = slice(32 * c, 32 * c + 32)
+            for part in range(2):
+                for k1 in (2 * j, 2 * j + 1):
+                    high, low = parts[k1][part]
+                    rows.append(jnp.concatenate((high[cut], low[cut]), 1))
+        sums = halves_added(dot_nt(table, jnp.concatenate(rows, 0)))
+        turned = [pltpu.roll(sums[64:, 128 * c : 128 * c + 128], 64, axis=1) for c in range(3)]
+        result = sums[:64] + jnp.concatenate(turned, 1) * sign
         for c in range(3):
             for t in range(8):
                 first = 384 * (j // 2) + 24 * (j % 2) + 48 * t + c
                 out_ref[pl.ds(first, 8, stride=3), :] = result[8 * t : 8 * t + 8, 128 * c : 128 * c + 128]
 
 
-def middle_front_kernel(anchor, band_hbm, r_ref, over_px_ref, front_tw_ref, within_ref, out_ref, band_ref, sem):
+def middle_front_kernel(anchor, band_hbm, r_ref, over_px_ref, front_tw_ref, within_ref, out_ref, packed_ref, band_ref, sem):
     band_copy = pltpu.make_async_copy(band_hbm, band_ref, sem)
     band_copy.start()
     data = jnp.concatenate([r_ref[pl.ds(c, 256, stride=3), :] for c in range(3)], 1)
@@ -230,13 +230,22 @@
         if left != right:
             values.append(lr * ri - li * rr)
         for value in values:
-            out_ref[64 * place : 64 * place + 64, :] = dot_nn(jnp.concatenate(split(value), 1), select) * scale
+            sums = dot_nn(jnp.concatenate(split(value), 1), select) * scale
+            out_ref[64 * place : 64 * place + 64, :] = sums
+            packed_ref[32 * place : 32 * place + 32, :] = jnp.where(lane64[:32] < 64, sums[:32], sums[32:])
             place += 1
 
 
 def middle_back_kernel(core, own_ref, got_ref, back_ref, back_tw_ref, final_ref, out_ref):
     first_core = core == 0
     zeros = jnp.zeros((32, 128), F32)
+    first_half = lax.broadcasted_iota(jnp.int32, (32, 128), 1) < 64
+    own, got = [], []
+    for place in range(9):
+        packed = got_ref[32 * place : 32 * place + 32, :]
+        turned = pltpu.roll(packed, 64, axis=1)
+        got.append((jnp.where(first_half, packed, turned), jnp.where(first_half, turned, packed)))
+        own.append([own_ref[64 * place + 32 * k : 64 * place + 32 * k + 32, :] for k in range(2)])
     columns = []
     for g in range(2):
         for k in range(2):
@@ -246,9 +255,8 @@
                     if part == 1 and left == right:
                         pieces.append(zeros)
                         continue
-                    rows = slice(64 * place + 32 * k, 64 * place + 32 * k + 32)
-                    own, got = own_ref[rows, :], got_ref[rows, :]
-                    pieces.append(jnp.where(first_core, own, got) if g == 0 else jnp.where(first_core, got, own))
+                    two = (own[place][k], got[place][k])
+                    pieces.append(jnp.where(first_core, two[g], two[1 - g]))
                     place += 1
             for sp in range(3):
                 columns.append(jnp.concatenate(pieces[4 * sp : 4 * sp + 4], 0))
@@ -330,12 +338,12 @@
 VMEM, HBM = pltpu.VMEM, pltpu.HBM
 
 
-def call(kernel, out_shape, in_specs, name, out_space=VMEM, scratch=()):
+def call(kernel, out_rows, in_specs, name, out_space=VMEM, scratch=()):
     return pl.pallas_call(
         kernel,
-        out_shape=jax.ShapeDtypeStruct(out_shape, F32),
+        out_shape=jax.tree.map(lambda rows: jax.ShapeDtypeStruct((rows, 128), F32), out_rows),
         in_specs=in_specs,
-        out_specs=pl.BlockSpec(memory_space=out_space),
+        out_specs=jax.tree.map(lambda rows: pl.BlockSpec(memory_space=out_space), out_rows),
         scratch_shapes=list(scratch),
         name=name,
         compiler_params=pltpu.CompilerParams(vmem_limit_bytes=16 * 1024 * 1024),
@@ -349,7 +357,7 @@
 def run_span_forward(velocity):
     twiddle, table = span_forward_tables()
     scratch = (VMEM((768, 128), F32), VMEM(twiddle.shape, F32), VMEM(table.shape, BF16), pltpu.SemaphoreType.DMA((3,)))
-    run = call(span_forward_kernel, (768, 128), spaces(HBM, HBM, HBM), "span_forward", scratch=scratch)
+    run = call(span_forward_kernel, 768, spaces(HBM, HBM, HBM), "span_forward", scratch=scratch)
     return run(in_hbm(velocity), in_hbm(twiddle), in_hbm(table))
 
 
@@ -361,7 +369,7 @@
         middle_front_kernel(at_anchor, *refs)
 
     scratch = (pltpu.SMEM((8,), jnp.int32), pltpu.SemaphoreType.DMA)
-    run = call(kernel, (576, 128), spaces(HBM, *[VMEM] * 4), "middle_front", scratch=scratch)
+    run = call(kernel, (576, 288), spaces(HBM, *[VMEM] * 4), "middle_front", scratch=scratch)
     return run(in_hbm(band_of), received, *middle_tables()[0])
 
 
@@ -369,20 +377,20 @@
     def kernel(*refs):
         middle_back_kernel(lax.axis_index("core") if core is None else core, *refs)
 
-    return call(kernel, (384, 128), spaces(*[VMEM] * 5), "middle_back")(own, got, *middle_tables()[1])
+    return call(kernel, 384, spaces(*[VMEM] * 5), "middle_back")(own, got, *middle_tables()[1])
 
 
 def run_span_inverse(received):
     scratch = (VMEM((384, 128), F32), pltpu.SemaphoreType.DMA((3,)))
-    run = call(span_inverse_kernel, (384, 128), spaces(VMEM, VMEM, VMEM), "span_inverse", HBM, scratch)
+    run = call(span_inverse_kernel, 384, spaces(VMEM, VMEM, VMEM), "span_inverse", HBM, scratch)
     return run(received, *span_inverse_tables())
 
 
 def per_device(velocity, band_of):
     sent = run_span_forward(velocity.reshape(768, 128))
     received = lax.all_to_all(sent.reshape(256, 1, 384), ("q", "core", "py"), 0, 0, tiled=True)
-    own = run_middle_front(received.reshape(768, 128), band_of)
-    got = lax.ppermute(own, "core", ((0, 1), (1, 0)))
+    own, packed = run_middle_front(received.reshape(768, 128), band_of)
+    got = lax.ppermute(packed, "core", ((0, 1), (1, 0)))
     back = run_middle_back(own, got)
     gathered = lax.all_to_all(back.reshape(128, 1, 384), ("q", "py"), 0, 0, tiled=True)
     out = run_span_inverse(gathered.reshape(384, 128))

time: 58.3 us -> 58.4 us (level)
  no operation moved by 1% of the time
where the time goes in v5:
time: 58.4 us; the launch traced here: 58.2 us
  blocking collectives  51.5 us (88%)
  Pallas kernels  4.86 us (8%)
  waiting for transfers between devices  1.01 us (2%)
  starting transfers between devices  0.74 us (1%)
    all_to_all x1, blocking collectives, per_device(): lax.all_to_all(sent.reshape(256, 1, 384), ('q', 'core', 'py'), 0, 0, tile...  33.9 us
    all_to_all x1, blocking collectives, per_device(): lax.all_to_all(back.reshape(128, 1, 384), ('q', 'py'), 0, 0, tiled=True)  17.6 us
    pallas_call x1, Pallas kernels, run_span_forward(): return run(in_hbm(velocity), in_hbm(twiddle), in_hbm(table))  1.68 us
    pallas_call x1, Pallas kernels, run_middle_front(): return run(in_hbm(band_of), received, *middle_tables()[0])  1.17 us
  transfers between devices with their start and end apart: 1, of which 1 were waited for; matrix products, arithmetic and copies ran while one was open for 0% of the time, Pallas kernels for 0%

profile of v5, /device:TPU:1, one launch (start us, length us, event | category | flops | bytes accessed | tf_op | source)
XLA Modules:
  0.0 58.2 jit_solution(10871889111208030566)
XLA Ops:
  0.0 0.0 copy-start.2
  0.0 1.7 %span_forward.1 = f32[768,128]{1,0:T(8,128)S(1)} custom-call(f32[768,128]{1,0:T(8,128)} %bitcast.14, f32[16,128]{1,0:T(8,128)} %constant.18.clone.twiddle_hbm.twiddle_ref, bf16[256,256]{1,0:T(8,128)(2,1)} %constant.19.clone.table_hbm), custom_call_target="tpu_custom_call" | custom-call | tf_op jit(solution)/shard_map/span_forward/pallas_call | solution.py:361
  1.7 0.0 copy-start
  1.7 0.0 copy-start.5
  1.7 33.9 %all_to_all.10 = f32[256,1,384]{2,1,0:T(1,128)S(1)} all-to-all(f32[256,1,384]{2,1,0:T(1,128)S(1)} %bitcast.10), channel_id=1, replica_groups=mesh['q'=16,'core'=2,'py'=8] {'q','core','py'}, dimensions={0} | all-to-all | bytes 786432 | tf_op jit(solution)/shard_map/all_to_all | solution.py:391
  35.6 0.0 copy-done.2
  35.6 0.0 copy-done
  35.6 0.0 copy-done.5
  35.6 0.0 copy-start.3
  35.7 0.0 copy-start.4
  35.7 0.0 copy-start.7
  35.7 1.2 %middle_front.1 = (f32[576,128]{1,0:T(8,128)S(1)}, f32[288,128]{1,0:T(8,128)S(1)}) custom-call(s32[8]{0:T(128)} %refs_0_.1, f32[768,128]{1,0:T(8,128)S(1)} %bitcast.11, bf16[256,768]{1,0:T(8,128)(2,1)S(1)} %copy-done.2, f32[1024,128]{1,0:T(8,128)S(1)} %copy-done, bf16[256,256]{1,0:T(8,128)(2,1)S(1)} %copy-done.5), custom_call_target="tpu_custom_call" | custom-call | tf_op jit(solution)/shard_map/middle_front/pallas_call | solution.py:373
  36.9 0.7 %collective-permute-start = (f32[288,128]{1,0:T(8,128)S(1)}, f32[288,128]{1,0:T(8,128)S(1)}, u32[]{:S(2)}, u32[]{:S(2)}) collective-permute-start(f32[288,128]{1,0:T(8,128)S(1)} %get-tuple-element.8), channel_id=1, source_target_pairs={{0,8},{8,0},{1,9},{9,1},{2,10},{10,2},{3,11},{11,3},{4,12},{12,4},... | collective-permute-start | bytes 442376 | tf_op jit(solution)/shard_map/ppermute | solution.py:393
  37.6 1.0 %collective-permute-done.refs_1_ = f32[288,128]{1,0:T(8,128)S(1)} collective-permute-done((f32[288,128]{1,0:T(8,128)S(1)}, f32[288,128]{1,0:T(8,128)S(1)}, u32[]{:S(2)}, u32[]{:S(2)}) %collective-permute-start) | collective-permute-done | bytes 147488 | tf_op jit(solution)/shard_map/ppermute | solution.py:393
  38.6 0.0 copy-done.3
  38.6 0.0 copy-done.4
  38.6 0.0 copy-done.7
  38.6 0.0 copy-start.6
  38.6 0.9 %middle_back.1 = f32[384,128]{1,0:T(8,128)S(1)} custom-call(f32[576,128]{1,0:T(8,128)S(1)} %get-tuple-element.7.refs_0_, f32[288,128]{1,0:T(8,128)S(1)} %collective-permute-done.refs_1_, bf16[256,256]{1,0:T(8,128)(2,1)S(1)} %copy-done.4, f32[256,128]{1,0:T(8,128)S(1)} %copy-done.3, bf16[64,256]{1,0:T(8,128)(2,1)S(1)} %copy-done.7), custom_call_target="tpu_custom_call" | custom-call | tf_op jit(solution)/shard_map/middle_back/pallas_call | solution.py:380
  39.5 0.0 copy-start.1
  39.5 17.6 %all_to_all.11 = f32[128,1,384]{2,1,0:T(1,128)S(1)} all-to-all(f32[128,1,384]{2,1,0:T(1,128)S(1)} %bitcast.12), channel_id=1, replica_groups=mesh['q'=16,'core'=2,'py'=8] {'q','py'}, dimensions={0} | all-to-all | bytes 393216 | tf_op jit(solution)/shard_map/all_to_all | solution.py:395
  57.1 0.0 copy-done.6
  57.1 0.0 copy-done.1
  57.1 1.1 %span_inverse.1 = f32[384,128]{1,0:T(8,128)} custom-call(f32[384,128]{1,0:T(8,128)S(1)} %bitcast.13, bf16[384,512]{1,0:T(8,128)(2,1)S(1)} %copy-done.1, f32[16,128]{1,0:T(8,128)S(1)} %copy-done.6), custom_call_target="tpu_custom_call" | custom-call | tf_op jit(solution)/shard_map/span_inverse/pallas_call | solution.py:386
Async XLA Ops:
  0.0 35.6 %copy-start.2 = (bf16[256,768]{1,0:T(8,128)(2,1)S(1)}, bf16[256,768]{1,0:T(8,128)(2,1)}, u32[]{:S(2)}) copy-start(bf16[256,768]{1,0:T(8,128)(2,1)} %constant.20.clone.refs_2_) | copy-start | bytes 1179652
  1.7 33.9 %copy-start = (f32[1024,128]{1,0:T(8,128)S(1)}, f32[1024,128]{1,0:T(8,128)}, u32[]{:S(2)}) copy-start(f32[1024,128]{1,0:T(8,128)} %constant.21.clone.refs_3_) | copy-start | bytes 1572868
  1.7 33.9 %copy-start.5 = (bf16[256,256]{1,0:T(8,128)(2,1)S(1)}, bf16[256,256]{1,0:T(8,128)(2,1)}, u32[]{:S(2)}) copy-start(bf16[256,256]{1,0:T(8,128)(2,1)} %constant.22.clone.refs_4_) | copy-start | bytes 393220
  35.6 3.0 %copy-start.3 = (f32[256,128]{1,0:T(8,128)S(1)}, f32[256,128]{1,0:T(8,128)}, u32[]{:S(2)}) copy-start(f32[256,128]{1,0:T(8,128)} %constant.24.clone.refs_3_) | copy-start | bytes 393220
  35.7 3.0 %copy-start.4 = (bf16[256,256]{1,0:T(8,128)(2,1)S(1)}, bf16[256,256]{1,0:T(8,128)(2,1)}, u32[]{:S(2)}) copy-start(bf16[256,256]{1,0:T(8,128)(2,1)} %constant.23.clone.refs_2_) | copy-start | bytes 393220
  35.7 3.0 %copy-start.7 = (bf16[64,256]{1,0:T(8,128)(2,1)S(1)}, bf16[64,256]{1,0:T(8,128)(2,1)}, u32[]{:S(2)}) copy-start(bf16[64,256]{1,0:T(8,128)(2,1)} %constant.25.clone.refs_4_) | copy-start | bytes 98308
  36.9 1.8 %collective-permute-start = (f32[288,128]{1,0:T(8,128)S(1)}, f32[288,128]{1,0:T(8,128)S(1)}, u32[]{:S(2)}, u32[]{:S(2)}) collective-permute-start(f32[288,128]{1,0:T(8,128)S(1)} %get-tuple-element.8), channel_id=1, source_target_pairs={{0,8},{8,0},{1,9},{9,1},{2,10},{10,2},{3,11},{11,3},{4,12},{12,4},... | collective-permute-start | bytes 442376 | tf_op jit(solution)/shard_map/ppermute | solution.py:393
  38.6 18.5 %copy-start.6 = (f32[16,128]{1,0:T(8,128)S(1)}, f32[16,128]{1,0:T(8,128)}, u32[]{:S(2)}) copy-start(f32[16,128]{1,0:T(8,128)} %constant.18.clone.twiddle_hbm.twiddle_ref) | copy-start | bytes 24580
  39.5 17.6 %copy-start.1 = (bf16[384,512]{1,0:T(8,128)(2,1)S(1)}, bf16[384,512]{1,0:T(8,128)(2,1)}, u32[]{:S(2)}) copy-start(bf16[384,512]{1,0:T(8,128)(2,1)} %constant.26.clone.table_ref) | copy-start | bytes 1179652

commit v6 on v4

--- a/solution.py
+++ b/solution.py
@@ -35,6 +35,18 @@
     return np.concatenate((parts[:, : 2 * width], np.concatenate((parts[:, 2 * width :], 0 * parts[:, :width]), 1)), 0)
 
 
+def order_of(axes):
+    sizes = dict(x=4, zh=4, core=2, zl=2, y=4)
+    places = np.indices([sizes[axis] for axis in axes]).reshape(len(axes), -1)
+    at = dict(zip(axes, places))
+    px = (at["x"] * 4 + at["zh"]) * 2 + at.get("core", 0)
+    return px, at["zl"] * 4 + at["y"], ((at["zh"] * 2 + at["zl"]) * 4 + at["y"]) * 4 + at["x"]
+
+
+FRONT_AXES = ("zh", "zl", "y", "x", "core")
+BACK_AXES = ("zl", "y", "zh", "x")
+
+
 def span_forward_tables():
     cos_tw, sin_tw = wave(np.arange(8), np.arange(128), 1024)
     twiddle = np.concatenate((cos_tw, sin_tw), 0).astype(np.float32)
@@ -47,7 +59,9 @@
     base = np.arange(32)
     cos32, sin32 = wave(base, base, 32)
     eye8 = np.eye(8)
-    over_px = three_part(np.concatenate((np.kron(cos32[:17], eye8), np.kron(-sin32[1:16], eye8)), 0))
+    over_px = np.concatenate((np.kron(cos32[:17], eye8), np.kron(-sin32[1:16], eye8)), 0)
+    px, py, _ = order_of(FRONT_AXES)
+    over_px = three_part(over_px[:, px * 8 + py])
     cos_tw, sin_tw = wave(base, base, 1024)
     spread = lambda t: np.repeat(np.tile(t, (1, 4)), 8, 0)
     turn_sign = np.where(base < 16, 1.0, -1.0)[:, None]
@@ -83,7 +97,7 @@
         back_twiddle[core, 1, :, :, :, 0] = s
         back_twiddle[core, 1, :, :, :, 1] = c
     back_twiddle = back_twiddle.reshape(256, 128).astype(np.float32)
-    cos16, sin16 = wave(np.arange(16), base, 16)
+    cos16, sin16 = wave(order_of(BACK_AXES)[0][:16] // 2, base, 16)
     final = paired(np.concatenate((np.kron(eye2, cos16), np.kron(eye2, sin16)), 1))
     return (over_px, front_twiddle, within), (back, back_twiddle, final)
 
@@ -91,7 +105,7 @@
 def span_inverse_tables():
     cos_t, sin_t = wave(np.arange(64), np.arange(128), 128)
     one = 2.0 * np.concatenate((cos_t, sin_t), 1)
-    table = three_part(np.kron(np.eye(2), one), 0)
+    table = three_part(np.kron(np.eye(2), one)[order_of(BACK_AXES)[2]], 0)
     cos_tw, sin_tw = wave(np.arange(8), np.arange(128), 1024)
     return table, np.concatenate((cos_tw, sin_tw), 0).astype(np.float32)
 
@@ -173,9 +187,8 @@
             columns.append(jnp.concatenate(rows, 0))
         result = halves_added(dot_nt(table, columns[0])) + dot_nt(table[:64], columns[1])
         for c in range(3):
-            for t in range(8):
-                first = 384 * (j // 2) + 24 * (j % 2) + 48 * t + c
-                out_ref[pl.ds(first, 8, stride=3), :] = result[8 * t : 8 * t + 8, 128 * c : 128 * c + 128]
+            first = 384 * (j // 2) + 3 * (j % 2) + c
+            out_ref[pl.ds(first, 64, stride=6), :] = result[:, 128 * c : 128 * c + 128]
 
 
 def middle_front_kernel(anchor, band_hbm, r_ref, over_px_ref, front_tw_ref, within_ref, out_ref, band_ref, sem):
@@ -266,9 +279,9 @@
             im_rows.append(vr * t2 + vi * t1)
         rows = jnp.concatenate(split(jnp.concatenate(re_rows + im_rows, 0)), 1)
         out = halves_added(dot_nt(final_ref[...], jnp.concatenate((rows, rows[128:]), 0)))
-        out_ref[pl.ds(3 * py, 16, stride=24), :] = out[:16, :128]
-        out_ref[pl.ds(3 * py + 1, 16, stride=24), :] = jnp.where(lane < 64, out[:16, 128:], out[16:, 128:])
-        out_ref[pl.ds(3 * py + 2, 16, stride=24), :] = out[16:, :128]
+        out_ref[pl.ds(48 * py, 16, stride=3), :] = out[:16, :128]
+        out_ref[pl.ds(48 * py + 1, 16, stride=3), :] = jnp.where(lane < 64, out[:16, 128:], out[16:, 128:])
+        out_ref[pl.ds(48 * py + 2, 16, stride=3), :] = out[16:, :128]
 
 
 def span_inverse_kernel(r_ref, table_ref, twiddle_ref, out_hbm, out_ref, sems):
@@ -357,7 +370,7 @@
     def kernel(*refs):
         at_anchor = anchor
         if anchor is None:
-            at_anchor = lax.axis_index("q") + lax.axis_index("core") + lax.axis_index("py") == 0
+            at_anchor = sum(lax.axis_index(axis) for axis in FRONT_AXES) == 0
         middle_front_kernel(at_anchor, *refs)
 
     scratch = (pltpu.SMEM((8,), jnp.int32), pltpu.SemaphoreType.DMA)
@@ -380,17 +393,18 @@
 
 def per_device(velocity, band_of):
     sent = run_span_forward(velocity.reshape(768, 128))
-    received = lax.all_to_all(sent.reshape(256, 1, 384), ("q", "core", "py"), 0, 0, tiled=True)
+    received = lax.all_to_all(sent.reshape(256, 1, 384), FRONT_AXES, 0, 0, tiled=True)
     own = run_middle_front(received.reshape(768, 128), band_of)
     got = lax.ppermute(own, "core", ((0, 1), (1, 0)))
     back = run_middle_back(own, got)
-    gathered = lax.all_to_all(back.reshape(128, 1, 384), ("q", "py"), 0, 0, tiled=True)
+    gathered = lax.all_to_all(back.reshape(128, 1, 384), BACK_AXES, 0, 0, tiled=True)
     out = run_span_inverse(gathered.reshape(384, 128))
     return out.reshape(6, 2, 8, 4, 128).transpose(0, 1, 3, 2, 4).reshape(6, 2, 4, 1024)
 
 
 def solution(mesh):
-    split_mesh = jax.sharding.Mesh(mesh.devices.reshape(16, 2, 8), ("q", "core", "py"))
-    in_specs = (P(None, ("q", "core"), "py", None), P())
-    out_specs = P(None, None, ("q", "core", "py"), None)
+    split_mesh = jax.sharding.Mesh(mesh.devices.reshape(4, 4, 2, 2, 4), ("x", "zh", "core", "zl", "y"))
+    px, py = ("x", "zh", "core"), ("zl", "y")
+    in_specs = (P(None, px, py, None), P())
+    out_specs = P(None, None, px + py, None)
     return jax.shard_map(per_device, mesh=split_mesh, in_specs=in_specs, out_specs=out_specs, check_vma=False)

time: 58.3 us -> 57.5 us (0.986)
  blocking collectives: 51.2 us -> 49.5 us
    all_to_all x2, blocking collectives: 51.2 us -> 49.5 us  [the longest x1 32.5 us: per_device(): lax.all_to_all(sent.reshape(256, 1, 384), FRONT_AXES, 0, 0, tiled=True)]
where the time goes in v6:
time: 57.5 us; the launch traced here: 56.8 us
  blocking collectives  49.5 us (86%)
  Pallas kernels  4.78 us (8%)
  waiting for transfers between devices  1.21 us (2%)
  starting transfers between devices  1.14 us (2%)
    all_to_all x1, blocking collectives, per_device(): lax.all_to_all(sent.reshape(256, 1, 384), FRONT_AXES, 0, 0, tiled=True)  32.5 us
    all_to_all x1, blocking collectives, per_device(): lax.all_to_all(back.reshape(128, 1, 384), BACK_AXES, 0, 0, tiled=True)  16.9 us
    pallas_call x1, Pallas kernels, run_span_forward(): return run(in_hbm(velocity), in_hbm(twiddle), in_hbm(table))  1.7 us
    ppermute x1, waiting for transfers between devices, per_device(): got = lax.ppermute(own, 'core', ((0, 1), (1, 0)))  1.21 us
    pallas_call x1, Pallas kernels, run_middle_front(): return run(in_hbm(band_of), received, *middle_tables()[0])  1.17 us
  transfers between devices with their start and end apart: 1, of which 1 were waited for; matrix products, arithmetic and copies ran while one was open for 0% of the time, Pallas kernels for 0%

profile of v6, /device:TPU:1, one launch (start us, length us, event | category | flops | bytes accessed | tf_op | source)
XLA Modules:
  0.0 56.8 jit_solution(8259117801252545435)
XLA Ops:
  0.0 0.0 copy-start.2
  0.0 1.7 %span_forward.1 = f32[768,128]{1,0:T(8,128)S(1)} custom-call(f32[768,128]{1,0:T(8,128)} %bitcast.14, f32[16,128]{1,0:T(8,128)} %constant.18.clone.twiddle_hbm.twiddle_ref, bf16[128,256]{1,0:T(8,128)(2,1)} %constant.19.clone.table_hbm), custom_call_target="tpu_custom_call" | custom-call | tf_op jit(solution)/shard_map/span_forward/pallas_call | solution.py:366
  1.7 0.0 copy-start
  1.7 0.0 copy-start.5
  1.7 32.5 %all_to_all.10 = f32[256,1,384]{2,1,0:T(1,128)S(1)} all-to-all(f32[256,1,384]{2,1,0:T(1,128)S(1)} %bitcast.11), channel_id=1, replica_groups=mesh['x'=4,'zh'=4,'core'=2,'zl'=2,'y'=4] {'zh','zl','y','x','core'}, dimensions={0} | all-to-all | bytes 786432 | tf_op jit(solution)/shard_map/all_to_all | solution.py:396
  34.3 0.0 copy-done.2
  34.3 0.0 copy-done
  34.3 0.0 copy-done.5
  34.3 0.0 copy-start.3
  34.3 0.0 copy-start.4
  34.3 0.0 copy-start.7
  34.3 1.2 %middle_front.1.refs_0_ = f32[576,128]{1,0:T(8,128)S(1)} custom-call(s32[8]{0:T(128)} %refs_0_.1, f32[768,128]{1,0:T(8,128)S(1)} %bitcast.10, bf16[256,768]{1,0:T(8,128)(2,1)S(1)} %copy-done.2, f32[1024,128]{1,0:T(8,128)S(1)} %copy-done, bf16[256,256]{1,0:T(8,128)(2,1)S(1)} %copy-done.5), custom_call_target="tpu_custom_call" | custom-call | tf_op jit(solution)/shard_map/middle_front/pallas_call | solution.py:378
  35.5 1.1 %collective-permute-start = (f32[576,128]{1,0:T(8,128)S(1)}, f32[576,128]{1,0:T(8,128)S(1)}, u32[]{:S(2)}, u32[]{:S(2)}) collective-permute-start(f32[576,128]{1,0:T(8,128)S(1)} %middle_front.1.refs_0_), channel_id=1, source_target_pairs={{0,8},{8,0},{1,9},{9,1},{2,10},{10,2},{3,11},{11,3},{4,12},{12,4},... | collective-permute-start | bytes 884744 | tf_op jit(solution)/shard_map/ppermute | solution.py:398
  36.6 1.2 %collective-permute-done.refs_1_ = f32[576,128]{1,0:T(8,128)S(1)} collective-permute-done((f32[576,128]{1,0:T(8,128)S(1)}, f32[576,128]{1,0:T(8,128)S(1)}, u32[]{:S(2)}, u32[]{:S(2)}) %collective-permute-start) | collective-permute-done | bytes 294944 | tf_op jit(solution)/shard_map/ppermute | solution.py:398
  37.9 0.0 copy-done.3
  37.9 0.0 copy-done.4
  37.9 0.0 copy-done.7
  37.9 0.0 copy-start.6
  37.9 0.8 %middle_back.1 = f32[384,128]{1,0:T(8,128)S(1)} custom-call(f32[576,128]{1,0:T(8,128)S(1)} %middle_front.1.refs_0_, f32[576,128]{1,0:T(8,128)S(1)} %collective-permute-done.refs_1_, bf16[256,256]{1,0:T(8,128)(2,1)S(1)} %copy-done.4, f32[256,128]{1,0:T(8,128)S(1)} %copy-done.3, bf16[64,256]{1,0:T(8,128)(2,1)S(1)} %copy-done.7), custom_call_target="tpu_custom_call" | custom-call | tf_op jit(solution)/shard_map/middle_back/pallas_call | solution.py:385
  38.7 0.0 copy-start.1
  38.7 16.9 %all_to_all.11 = f32[128,1,384]{2,1,0:T(1,128)S(1)} all-to-all(f32[128,1,384]{2,1,0:T(1,128)S(1)} %bitcast.13), channel_id=1, replica_groups=mesh['x'=4,'zh'=4,'core'=2,'zl'=2,'y'=4] {'zl','y','zh','x'}, dimensions={0} | all-to-all | bytes 393216 | tf_op jit(solution)/shard_map/all_to_all | solution.py:400
  55.6 0.0 copy-done.6
  55.6 0.0 copy-done.1
  55.6 1.1 %span_inverse.1 = f32[384,128]{1,0:T(8,128)} custom-call(f32[384,128]{1,0:T(8,128)S(1)} %bitcast.12, bf16[384,512]{1,0:T(8,128)(2,1)S(1)} %copy-done.1, f32[16,128]{1,0:T(8,128)S(1)} %copy-done.6), custom_call_target="tpu_custom_call" | custom-call | tf_op jit(solution)/shard_map/span_inverse/pallas_call | solution.py:391
Async XLA Ops:
  0.0 34.3 %copy-start.2 = (bf16[256,768]{1,0:T(8,128)(2,1)S(1)}, bf16[256,768]{1,0:T(8,128)(2,1)}, u32[]{:S(2)}) copy-start(bf16[256,768]{1,0:T(8,128)(2,1)} %constant.20.clone.refs_2_) | copy-start | bytes 1179652
  1.7 32.6 %copy-start = (f32[1024,128]{1,0:T(8,128)S(1)}, f32[1024,128]{1,0:T(8,128)}, u32[]{:S(2)}) copy-start(f32[1024,128]{1,0:T(8,128)} %constant.21.clone.refs_3_) | copy-start | bytes 1572868
  1.7 32.6 %copy-start.5 = (bf16[256,256]{1,0:T(8,128)(2,1)S(1)}, bf16[256,256]{1,0:T(8,128)(2,1)}, u32[]{:S(2)}) copy-start(bf16[256,256]{1,0:T(8,128)(2,1)} %constant.22.clone.refs_4_) | copy-start | bytes 393220
  34.3 3.6 %copy-start.3 = (f32[256,128]{1,0:T(8,128)S(1)}, f32[256,128]{1,0:T(8,128)}, u32[]{:S(2)}) copy-start(f32[256,128]{1,0:T(8,128)} %constant.24.clone.refs_3_) | copy-start | bytes 393220
  34.3 3.6 %copy-start.4 = (bf16[256,256]{1,0:T(8,128)(2,1)S(1)}, bf16[256,256]{1,0:T(8,128)(2,1)}, u32[]{:S(2)}) copy-start(bf16[256,256]{1,0:T(8,128)(2,1)} %constant.23.clone.refs_2_) | copy-start | bytes 393220
  34.3 3.5 %copy-start.7 = (bf16[64,256]{1,0:T(8,128)(2,1)S(1)}, bf16[64,256]{1,0:T(8,128)(2,1)}, u32[]{:S(2)}) copy-start(bf16[64,256]{1,0:T(8,128)(2,1)} %constant.25.clone.refs_4_) | copy-start | bytes 98308
  35.5 2.3 %collective-permute-start = (f32[576,128]{1,0:T(8,128)S(1)}, f32[576,128]{1,0:T(8,128)S(1)}, u32[]{:S(2)}, u32[]{:S(2)}) collective-permute-start(f32[576,128]{1,0:T(8,128)S(1)} %middle_front.1.refs_0_), channel_id=1, source_target_pairs={{0,8},{8,0},{1,9},{9,1},{2,10},{10,2},{3,11},{11,3},{4,12},{12,4},... | collective-permute-start | bytes 884744 | tf_op jit(solution)/shard_map/ppermute | solution.py:398
  37.9 17.8 %copy-start.6 = (f32[16,128]{1,0:T(8,128)S(1)}, f32[16,128]{1,0:T(8,128)}, u32[]{:S(2)}) copy-start(f32[16,128]{1,0:T(8,128)} %constant.18.clone.twiddle_hbm.twiddle_ref) | copy-start | bytes 24580
  38.7 17.0 %copy-start.1 = (bf16[384,512]{1,0:T(8,128)(2,1)S(1)}, bf16[384,512]{1,0:T(8,128)(2,1)}, u32[]{:S(2)}) copy-start(bf16[384,512]{1,0:T(8,128)(2,1)} %constant.26.clone.table_ref) | copy-start | bytes 1179652

commit v7 on v6

--- a/solution.py
+++ b/solution.py
@@ -40,10 +40,10 @@
     places = np.indices([sizes[axis] for axis in axes]).reshape(len(axes), -1)
     at = dict(zip(axes, places))
     px = (at["x"] * 4 + at["zh"]) * 2 + at.get("core", 0)
-    return px, at["zl"] * 4 + at["y"], ((at["zh"] * 2 + at["zl"]) * 4 + at["y"]) * 4 + at["x"]
-
-
-FRONT_AXES = ("zh", "zl", "y", "x", "core")
+    return px, at["zl"] * 4 + at["y"], ((at["x"] * 4 + at["zh"]) * 2 + at["zl"]) * 4 + at["y"]
+
+
+FRONT_AXES = ("zh", "zl", "y", "core", "x")
 BACK_AXES = ("zl", "y", "zh", "x")
 
 
@@ -187,8 +187,9 @@
             columns.append(jnp.concatenate(rows, 0))
         result = halves_added(dot_nt(table, columns[0])) + dot_nt(table[:64], columns[1])
         for c in range(3):
-            first = 384 * (j // 2) + 3 * (j % 2) + c
-            out_ref[pl.ds(first, 64, stride=6), :] = result[:, 128 * c : 128 * c + 128]
+            for half in range(2):
+                first = 3 * (4 * (j % 2) + 2 * (j // 2) + half) + c
+                out_ref[pl.ds(first, 32, stride=24), :] = result[32 * half : 32 * half + 32, 128 * c : 128 * c + 128]
 
 
 def middle_front_kernel(anchor, band_hbm, r_ref, over_px_ref, front_tw_ref, within_ref, out_ref, band_ref, sem):

time: 57.5 us -> 57.7 us (level)
  starting transfers between devices: 1.14 us -> 0.09 us
  blocking collectives: 49.5 us -> 50.3 us
    ppermute x1, starting transfers between devices: 1.14 us -> 0.09 us  [per_device(): got = lax.ppermute(own, 'core', ((0, 1), (1, 0)))]
    all_to_all x1, blocking collectives: 16.9 us -> 17.6 us  [per_device(): lax.all_to_all(back.reshape(128, 1, 384), BACK_AXES, 0, 0, tiled=True)]
where the time goes in v7:
time: 57.7 us; the launch traced here: 56.9 us
  blocking collectives  50.3 us (87%)
  Pallas kernels  4.78 us (8%)
  waiting for transfers between devices  1.57 us (3%)
    all_to_all x1, blocking collectives, per_device(): lax.all_to_all(sent.reshape(256, 1, 384), FRONT_AXES, 0, 0, tiled=True)  32.8 us
    all_to_all x1, blocking collectives, per_device(): lax.all_to_all(back.reshape(128, 1, 384), BACK_AXES, 0, 0, tiled=True)  17.6 us
    pallas_call x1, Pallas kernels, run_span_forward(): return run(in_hbm(velocity), in_hbm(twiddle), in_hbm(table))  1.71 us
    ppermute x1, waiting for transfers between devices, per_device(): got = lax.ppermute(own, 'core', ((0, 1), (1, 0)))  1.57 us
    pallas_call x1, Pallas kernels, run_middle_front(): return run(in_hbm(band_of), received, *middle_tables()[0])  1.17 us
  transfers between devices with their start and end apart: 1, of which 1 were waited for; matrix products, arithmetic and copies ran while one was open for 0% of the time, Pallas kernels for 0%

profile of v7, /device:TPU:1, one launch (start us, length us, event | category | flops | bytes accessed | tf_op | source)
XLA Modules:
  0.0 56.9 jit_solution(6701382212347874878)
XLA Ops:
  0.0 0.0 copy-start.2
  0.0 1.7 %span_forward.1 = f32[768,128]{1,0:T(8,128)S(1)} custom-call(f32[768,128]{1,0:T(8,128)} %bitcast.14, f32[16,128]{1,0:T(8,128)} %constant.18.clone.twiddle_hbm.twiddle_ref, bf16[128,256]{1,0:T(8,128)(2,1)} %constant.19.clone.table_hbm), custom_call_target="tpu_custom_call" | custom-call | tf_op jit(solution)/shard_map/span_forward/pallas_call | solution.py:367
  1.7 0.0 copy-start
  1.7 0.0 copy-start.5
  1.7 32.8 %all_to_all.10 = f32[256,1,384]{2,1,0:T(1,128)S(1)} all-to-all(f32[256,1,384]{2,1,0:T(1,128)S(1)} %bitcast.11), channel_id=1, replica_groups=mesh['x'=4,'zh'=4,'core'=2,'zl'=2,'y'=4] {'zh','zl','y','core','x'}, dimensions={0} | all-to-all | bytes 786432 | tf_op jit(solution)/shard_map/all_to_all | solution.py:397
  34.5 0.0 copy-done.2
  34.5 0.0 copy-done
  34.5 0.0 copy-done.5
  34.5 0.0 copy-start.3
  34.5 0.0 copy-start.4
  34.5 0.0 copy-start.7
  34.5 1.2 %middle_front.1.refs_0_ = f32[576,128]{1,0:T(8,128)S(1)} custom-call(s32[8]{0:T(128)} %refs_0_.1, f32[768,128]{1,0:T(8,128)S(1)} %bitcast.10, bf16[256,768]{1,0:T(8,128)(2,1)S(1)} %copy-done.2, f32[1024,128]{1,0:T(8,128)S(1)} %copy-done, bf16[256,256]{1,0:T(8,128)(2,1)S(1)} %copy-done.5), custom_call_target="tpu_custom_call" | custom-call | tf_op jit(solution)/shard_map/middle_front/pallas_call | solution.py:379
  35.7 0.1 collective-permute-start
  35.8 1.6 %collective-permute-done.refs_1_ = f32[576,128]{1,0:T(8,128)S(1)} collective-permute-done((f32[576,128]{1,0:T(8,128)S(1)}, f32[576,128]{1,0:T(8,128)S(1)}, u32[]{:S(2)}, u32[]{:S(2)}) %collective-permute-start) | collective-permute-done | bytes 294944 | tf_op jit(solution)/shard_map/ppermute | solution.py:399
  37.4 0.0 copy-done.3
  37.4 0.0 copy-done.4
  37.4 0.0 copy-done.7
  37.4 0.0 copy-start.6
  37.4 0.8 %middle_back.1 = f32[384,128]{1,0:T(8,128)S(1)} custom-call(f32[576,128]{1,0:T(8,128)S(1)} %middle_front.1.refs_0_, f32[576,128]{1,0:T(8,128)S(1)} %collective-permute-done.refs_1_, bf16[256,256]{1,0:T(8,128)(2,1)S(1)} %copy-done.4, f32[256,128]{1,0:T(8,128)S(1)} %copy-done.3, bf16[64,256]{1,0:T(8,128)(2,1)S(1)} %copy-done.7), custom_call_target="tpu_custom_call" | custom-call | tf_op jit(solution)/shard_map/middle_back/pallas_call | solution.py:386
  38.2 0.0 copy-start.1
  38.2 17.6 %all_to_all.11 = f32[128,1,384]{2,1,0:T(1,128)S(1)} all-to-all(f32[128,1,384]{2,1,0:T(1,128)S(1)} %bitcast.13), channel_id=1, replica_groups=mesh['x'=4,'zh'=4,'core'=2,'zl'=2,'y'=4] {'zl','y','zh','x'}, dimensions={0} | all-to-all | bytes 393216 | tf_op jit(solution)/shard_map/all_to_all | solution.py:401
  55.8 0.0 copy-done.6
  55.8 0.0 copy-done.1
  55.8 1.1 %span_inverse.1 = f32[384,128]{1,0:T(8,128)} custom-call(f32[384,128]{1,0:T(8,128)S(1)} %bitcast.12, bf16[384,512]{1,0:T(8,128)(2,1)S(1)} %copy-done.1, f32[16,128]{1,0:T(8,128)S(1)} %copy-done.6), custom_call_target="tpu_custom_call" | custom-call | tf_op jit(solution)/shard_map/span_inverse/pallas_call | solution.py:392
Async XLA Ops:
  0.0 34.5 %copy-start.2 = (bf16[256,768]{1,0:T(8,128)(2,1)S(1)}, bf16[256,768]{1,0:T(8,128)(2,1)}, u32[]{:S(2)}) copy-start(bf16[256,768]{1,0:T(8,128)(2,1)} %constant.20.clone.refs_2_) | copy-start | bytes 1179652
  1.7 32.8 %copy-start = (f32[1024,128]{1,0:T(8,128)S(1)}, f32[1024,128]{1,0:T(8,128)}, u32[]{:S(2)}) copy-start(f32[1024,128]{1,0:T(8,128)} %constant.21.clone.refs_3_) | copy-start | bytes 1572868
  1.7 32.8 %copy-start.5 = (bf16[256,256]{1,0:T(8,128)(2,1)S(1)}, bf16[256,256]{1,0:T(8,128)(2,1)}, u32[]{:S(2)}) copy-start(bf16[256,256]{1,0:T(8,128)(2,1)} %constant.22.clone.refs_4_) | copy-start | bytes 393220
  34.5 2.9 %copy-start.3 = (f32[256,128]{1,0:T(8,128)S(1)}, f32[256,128]{1,0:T(8,128)}, u32[]{:S(2)}) copy-start(f32[256,128]{1,0:T(8,128)} %constant.24.clone.refs_3_) | copy-start | bytes 393220
  34.5 2.9 %copy-start.4 = (bf16[256,256]{1,0:T(8,128)(2,1)S(1)}, bf16[256,256]{1,0:T(8,128)(2,1)}, u32[]{:S(2)}) copy-start(bf16[256,256]{1,0:T(8,128)(2,1)} %constant.23.clone.refs_2_) | copy-start | bytes 393220
  34.5 2.9 %copy-start.7 = (bf16[64,256]{1,0:T(8,128)(2,1)S(1)}, bf16[64,256]{1,0:T(8,128)(2,1)}, u32[]{:S(2)}) copy-start(bf16[64,256]{1,0:T(8,128)(2,1)} %constant.25.clone.refs_4_) | copy-start | bytes 98308
  35.7 1.7 %collective-permute-start = (f32[576,128]{1,0:T(8,128)S(1)}, f32[576,128]{1,0:T(8,128)S(1)}, u32[]{:S(2)}, u32[]{:S(2)}) collective-permute-start(f32[576,128]{1,0:T(8,128)S(1)} %middle_front.1.refs_0_), channel_id=1, source_target_pairs={{0,8},{8,0},{1,9},{9,1},{2,10},{10,2},{3,11},{11,3},{4,12},{12,4},... | collective-permute-start | bytes 884744 | tf_op jit(solution)/shard_map/ppermute | solution.py:399
  37.4 18.4 %copy-start.6 = (f32[16,128]{1,0:T(8,128)S(1)}, f32[16,128]{1,0:T(8,128)}, u32[]{:S(2)}) copy-start(f32[16,128]{1,0:T(8,128)} %constant.18.clone.twiddle_hbm.twiddle_ref) | copy-start | bytes 24580
  38.2 17.6 %copy-start.1 = (bf16[384,512]{1,0:T(8,128)(2,1)S(1)}, bf16[384,512]{1,0:T(8,128)(2,1)}, u32[]{:S(2)}) copy-start(bf16[384,512]{1,0:T(8,128)(2,1)} %constant.26.clone.table_ref) | copy-start | bytes 1179652

commit v8 on v6

--- a/solution.py
+++ b/solution.py
@@ -247,37 +247,49 @@
             place += 1
 
 
-def middle_back_kernel(core, own_ref, got_ref, back_ref, back_tw_ref, final_ref, out_ref):
-    first_core = core == 0
+def back_rows(core, banded_ref, back_ref, back_tw_ref):
     zeros = jnp.zeros((32, 128), F32)
     columns = []
-    for g in range(2):
-        for k in range(2):
-            place, pieces = 0, []
-            for left, right in PAIR_LIST:
-                for part in range(2):
-                    if part == 1 and left == right:
-                        pieces.append(zeros)
-                        continue
-                    rows = slice(64 * place + 32 * k, 64 * place + 32 * k + 32)
-                    own, got = own_ref[rows, :], got_ref[rows, :]
-                    pieces.append(jnp.where(first_core, own, got) if g == 0 else jnp.where(first_core, got, own))
-                    place += 1
-            for sp in range(3):
-                columns.append(jnp.concatenate(pieces[4 * sp : 4 * sp + 4], 0))
+    for k in range(2):
+        place, pieces = 0, []
+        for left, right in PAIR_LIST:
+            for part in range(2):
+                if part == 1 and left == right:
+                    pieces.append(zeros)
+                    continue
+                pieces.append(banded_ref[64 * place + 32 * k : 64 * place + 32 * k + 32, :])
+                place += 1
+        for sp in range(3):
+            columns.append(jnp.concatenate(pieces[4 * sp : 4 * sp + 4], 0))
     v = halves_added(dot_nn(back_ref[...], jnp.concatenate(split(jnp.concatenate(columns, 1)), 0)))
-    lane = lax.broadcasted_iota(jnp.int32, (16, 128), 1)
     twiddle_row = pl.multiple_of(core * 128, 128)
+    blocks = []
     for py in range(8):
         t1 = back_tw_ref[pl.ds(twiddle_row + 8 * py, 8), :]
         t2 = back_tw_ref[pl.ds(twiddle_row + 64 + 8 * py, 8), :]
         re_rows, im_rows = [], []
-        for column in range(12):
+        for column in range(6):
             cut = slice(128 * column, 128 * column + 128)
             vr, vi = v[16 * py : 16 * py + 8, cut], v[16 * py + 8 : 16 * py + 16, cut]
             re_rows.append(vr * t1 - vi * t2)
             im_rows.append(vr * t2 + vi * t1)
-        rows = jnp.concatenate(split(jnp.concatenate(re_rows + im_rows, 0)), 1)
+        blocks.append(jnp.concatenate(split(jnp.concatenate(re_rows + im_rows, 0)), 1))
+    return blocks
+
+
+def middle_own_kernel(core, own_ref, back_ref, back_tw_ref, out_ref):
+    for py, block in enumerate(back_rows(core, own_ref, back_ref, back_tw_ref)):
+        out_ref[96 * py : 96 * py + 96, :] = block
+
+
+def middle_back_kernel(core, rows_ref, got_ref, back_ref, back_tw_ref, final_ref, out_ref):
+    first_core = core == 0
+    lane = lax.broadcasted_iota(jnp.int32, (16, 128), 1)
+    for py, got in enumerate(back_rows(core, got_ref, back_ref, back_tw_ref)):
+        own = rows_ref[96 * py : 96 * py + 96, :]
+        first = jnp.where(first_core, own, got)
+        second = jnp.where(first_core, got, own)
+        rows = jnp.concatenate((first[:48], second[:48], first[48:], second[48:]), 0)
         out = halves_added(dot_nt(final_ref[...], jnp.concatenate((rows, rows[128:]), 0)))
         out_ref[pl.ds(48 * py, 16, stride=3), :] = out[:16, :128]
         out_ref[pl.ds(48 * py + 1, 16, stride=3), :] = jnp.where(lane < 64, out[:16, 128:], out[16:, 128:])
@@ -343,10 +355,10 @@
 VMEM, HBM = pltpu.VMEM, pltpu.HBM
 
 
-def call(kernel, out_shape, in_specs, name, out_space=VMEM, scratch=()):
+def call(kernel, out_shape, in_specs, name, out_space=VMEM, scratch=(), dtype=F32):
     return pl.pallas_call(
         kernel,
-        out_shape=jax.ShapeDtypeStruct(out_shape, F32),
+        out_shape=jax.ShapeDtypeStruct(out_shape, dtype),
         in_specs=in_specs,
         out_specs=pl.BlockSpec(memory_space=out_space),
         scratch_shapes=list(scratch),
@@ -378,11 +390,19 @@
     return run(in_hbm(band_of), received, *middle_tables()[0])
 
 
-def run_middle_back(own, got, core=None):
+def run_middle_own(own, core=None):
+    def kernel(*refs):
+        middle_own_kernel(lax.axis_index("core") if core is None else core, *refs)
+
+    back, twiddle, _ = middle_tables()[1]
+    return call(kernel, (768, 256), spaces(*[VMEM] * 3), "middle_own", dtype=BF16)(own, back, twiddle)
+
+
+def run_middle_back(rows, got, core=None):
     def kernel(*refs):
         middle_back_kernel(lax.axis_index("core") if core is None else core, *refs)
 
-    return call(kernel, (384, 128), spaces(*[VMEM] * 5), "middle_back")(own, got, *middle_tables()[1])
+    return call(kernel, (384, 128), spaces(*[VMEM] * 5), "middle_back")(rows, got, *middle_tables()[1])
 
 
 def run_span_inverse(received):
@@ -396,7 +416,7 @@
     received = lax.all_to_all(sent.reshape(256, 1, 384), FRONT_AXES, 0, 0, tiled=True)
     own = run_middle_front(received.reshape(768, 128), band_of)
     got = lax.ppermute(own, "core", ((0, 1), (1, 0)))
-    back = run_middle_back(own, got)
+    back = run_middle_back(run_middle_own(own), got)
     gathered = lax.all_to_all(back.reshape(128, 1, 384), BACK_AXES, 0, 0, tiled=True)
     out = run_span_inverse(gathered.reshape(384, 128))
     return out.reshape(6, 2, 8, 4, 128).transpose(0, 1, 3, 2, 4).reshape(6, 2, 4, 1024)

time: 57.5 us -> 57.4 us (level)
  transfers between devices with their start and end apart: 1 -> 1, of which waited for: 1 -> 1; matrix products, arithmetic and copies ran while one was open for 0% -> 0% of each run, Pallas kernels for 0% -> 1%
where the time goes in v8:
time: 57.4 us; the launch traced here: 56.6 us
  blocking collectives  49.5 us (86%)
  Pallas kernels  4.98 us (9%)
  starting transfers between devices  1.14 us (2%)
  waiting for transfers between devices  0.9 us (2%)
    all_to_all x1, blocking collectives, per_device(): lax.all_to_all(sent.reshape(256, 1, 384), FRONT_AXES, 0, 0, tiled=True)  32.5 us
    all_to_all x1, blocking collectives, per_device(): lax.all_to_all(back.reshape(128, 1, 384), BACK_AXES, 0, 0, tiled=True)  16.9 us
    pallas_call x1, Pallas kernels, run_span_forward(): return run(in_hbm(velocity), in_hbm(twiddle), in_hbm(table))  1.7 us
    pallas_call x1, Pallas kernels, run_middle_front(): return run(in_hbm(band_of), received, *middle_tables()[0])  1.17 us
  transfers between devices with their start and end apart: 1, of which 1 were waited for; matrix products, arithmetic and copies ran while one was open for 0% of the time, Pallas kernels for 1%

profile of v8, /device:TPU:1, one launch (start us, length us, event | category | flops | bytes accessed | tf_op | source)
XLA Modules:
  0.0 56.6 jit_solution(18089305634944139113)
XLA Ops:
  0.0 0.0 copy-start.4
  0.0 1.7 %span_forward.1 = f32[768,128]{1,0:T(8,128)S(1)} custom-call(f32[768,128]{1,0:T(8,128)} %bitcast.14, f32[16,128]{1,0:T(8,128)} %constant.18.clone.twiddle_hbm.twiddle_ref, bf16[128,256]{1,0:T(8,128)(2,1)} %constant.19.clone.table_hbm), custom_call_target="tpu_custom_call" | custom-call | tf_op jit(solution)/shard_map/span_forward/pallas_call | solution.py:378
  1.7 0.0 copy-start
  1.7 0.0 copy-start.5
  1.7 32.5 %all_to_all.10 = f32[256,1,384]{2,1,0:T(1,128)S(1)} all-to-all(f32[256,1,384]{2,1,0:T(1,128)S(1)} %bitcast.11), channel_id=1, replica_groups=mesh['x'=4,'zh'=4,'core'=2,'zl'=2,'y'=4] {'zh','zl','y','x','core'}, dimensions={0} | all-to-all | bytes 786432 | tf_op jit(solution)/shard_map/all_to_all | solution.py:416
  34.3 0.0 copy-done.4
  34.3 0.0 copy-done
  34.3 0.0 copy-done.5
  34.3 0.0 copy-start.1
  34.3 0.0 copy-start.2
  34.3 1.2 %middle_front.1.refs_0_ = f32[576,128]{1,0:T(8,128)S(1)} custom-call(s32[8]{0:T(128)} %refs_0_.1, f32[768,128]{1,0:T(8,128)S(1)} %bitcast.10, bf16[256,768]{1,0:T(8,128)(2,1)S(1)} %copy-done.4, f32[1024,128]{1,0:T(8,128)S(1)} %copy-done, bf16[256,256]{1,0:T(8,128)(2,1)S(1)} %copy-done.5), custom_call_target="tpu_custom_call" | custom-call | tf_op jit(solution)/shard_map/middle_front/pallas_call | solution.py:390
  35.5 0.0 copy-start.7
  35.5 1.1 %collective-permute-start = (f32[576,128]{1,0:T(8,128)S(1)}, f32[576,128]{1,0:T(8,128)S(1)}, u32[]{:S(2)}, u32[]{:S(2)}) collective-permute-start(f32[576,128]{1,0:T(8,128)S(1)} %middle_front.1.refs_0_), channel_id=1, source_target_pairs={{0,8},{8,0},{1,9},{9,1},{2,10},{10,2},{3,11},{11,3},{4,12},{12,4},... | collective-permute-start | bytes 884744 | tf_op jit(solution)/shard_map/ppermute | solution.py:418
  36.6 0.0 copy-done.1
  36.6 0.0 copy-done.2
  36.6 0.3 middle_own.1.refs_0_
  37.0 0.9 %collective-permute-done.refs_1_ = f32[576,128]{1,0:T(8,128)S(1)} collective-permute-done((f32[576,128]{1,0:T(8,128)S(1)}, f32[576,128]{1,0:T(8,128)S(1)}, u32[]{:S(2)}, u32[]{:S(2)}) %collective-permute-start) | collective-permute-done | bytes 294944 | tf_op jit(solution)/shard_map/ppermute | solution.py:418
  37.9 0.0 copy-done.7
  37.9 0.0 copy-start.6
  37.9 0.7 %middle_back.1 = f32[384,128]{1,0:T(8,128)S(1)} custom-call(bf16[768,256]{1,0:T(8,128)(2,1)S(1)} %middle_own.1.refs_0_, f32[576,128]{1,0:T(8,128)S(1)} %collective-permute-done.refs_1_, bf16[256,256]{1,0:T(8,128)(2,1)S(1)} %copy-done.2, f32[256,128]{1,0:T(8,128)S(1)} %copy-done.1, bf16[64,256]{1,0:T(8,128)(2,1)S(1)} %copy-done.7), custom_call_target="tpu_custom_call" | custom-call | tf_op jit(solution)/shard_map/middle_back/pallas_call | solution.py:405
  38.5 0.0 copy-start.3
  38.6 16.9 %all_to_all.11 = f32[128,1,384]{2,1,0:T(1,128)S(1)} all-to-all(f32[128,1,384]{2,1,0:T(1,128)S(1)} %bitcast.12), channel_id=1, replica_groups=mesh['x'=4,'zh'=4,'core'=2,'zl'=2,'y'=4] {'zl','y','zh','x'}, dimensions={0} | all-to-all | bytes 393216 | tf_op jit(solution)/shard_map/all_to_all | solution.py:420
  55.5 0.0 copy-done.6
  55.5 0.0 copy-done.3
  55.5 1.1 %span_inverse.1 = f32[384,128]{1,0:T(8,128)} custom-call(f32[384,128]{1,0:T(8,128)S(1)} %bitcast.13, bf16[384,512]{1,0:T(8,128)(2,1)S(1)} %copy-done.3, f32[16,128]{1,0:T(8,128)S(1)} %copy-done.6), custom_call_target="tpu_custom_call" | custom-call | tf_op jit(solution)/shard_map/span_inverse/pallas_call | solution.py:411
Async XLA Ops:
  0.0 34.3 %copy-start.4 = (bf16[256,768]{1,0:T(8,128)(2,1)S(1)}, bf16[256,768]{1,0:T(8,128)(2,1)}, u32[]{:S(2)}) copy-start(bf16[256,768]{1,0:T(8,128)(2,1)} %constant.20.clone.refs_2_) | copy-start | bytes 1179652
  1.7 32.6 %copy-start = (f32[1024,128]{1,0:T(8,128)S(1)}, f32[1024,128]{1,0:T(8,128)}, u32[]{:S(2)}) copy-start(f32[1024,128]{1,0:T(8,128)} %constant.21.clone.refs_3_) | copy-start | bytes 1572868
  1.7 32.6 %copy-start.5 = (bf16[256,256]{1,0:T(8,128)(2,1)S(1)}, bf16[256,256]{1,0:T(8,128)(2,1)}, u32[]{:S(2)}) copy-start(bf16[256,256]{1,0:T(8,128)(2,1)} %constant.22.clone.refs_4_) | copy-start | bytes 393220
  34.3 2.4 %copy-start.1 = (f32[256,128]{1,0:T(8,128)S(1)}, f32[256,128]{1,0:T(8,128)}, u32[]{:S(2)}) copy-start(f32[256,128]{1,0:T(8,128)} %constant.24.clone.refs_2_.refs_3_) | copy-start | bytes 393220
  34.3 2.3 %copy-start.2 = (bf16[256,256]{1,0:T(8,128)(2,1)S(1)}, bf16[256,256]{1,0:T(8,128)(2,1)}, u32[]{:S(2)}) copy-start(bf16[256,256]{1,0:T(8,128)(2,1)} %constant.23.clone.refs_1_.refs_2_) | copy-start | bytes 393220
  35.5 2.4 %copy-start.7 = (bf16[64,256]{1,0:T(8,128)(2,1)S(1)}, bf16[64,256]{1,0:T(8,128)(2,1)}, u32[]{:S(2)}) copy-start(bf16[64,256]{1,0:T(8,128)(2,1)} %constant.25.clone.refs_4_) | copy-start | bytes 98308
  35.5 2.3 %collective-permute-start = (f32[576,128]{1,0:T(8,128)S(1)}, f32[576,128]{1,0:T(8,128)S(1)}, u32[]{:S(2)}, u32[]{:S(2)}) collective-permute-start(f32[576,128]{1,0:T(8,128)S(1)} %middle_front.1.refs_0_), channel_id=1, source_target_pairs={{0,8},{8,0},{1,9},{9,1},{2,10},{10,2},{3,11},{11,3},{4,12},{12,4},... | collective-permute-start | bytes 884744 | tf_op jit(solution)/shard_map/ppermute | solution.py:418
  37.9 17.6 %copy-start.6 = (f32[16,128]{1,0:T(8,128)S(1)}, f32[16,128]{1,0:T(8,128)}, u32[]{:S(2)}) copy-start(f32[16,128]{1,0:T(8,128)} %constant.18.clone.twiddle_hbm.twiddle_ref) | copy-start | bytes 24580
  38.5 17.0 %copy-start.3 = (bf16[384,512]{1,0:T(8,128)(2,1)S(1)}, bf16[384,512]{1,0:T(8,128)(2,1)}, u32[]{:S(2)}) copy-start(bf16[384,512]{1,0:T(8,128)(2,1)} %constant.26.clone.table_ref) | copy-start | bytes 1179652

commit v9 on v8

--- a/solution.py
+++ b/solution.py
@@ -191,7 +191,7 @@
             out_ref[pl.ds(first, 64, stride=6), :] = result[:, 128 * c : 128 * c + 128]
 
 
-def middle_front_kernel(anchor, band_hbm, r_ref, over_px_ref, front_tw_ref, within_ref, out_ref, band_ref, sem):
+def middle_front_kernel(anchor, band_hbm, r_ref, over_px_ref, front_tw_ref, within_ref, out_ref, packed_ref, band_ref, sem):
     band_copy = pltpu.make_async_copy(band_hbm, band_ref, sem)
     band_copy.start()
     data = jnp.concatenate([r_ref[pl.ds(c, 256, stride=3), :] for c in range(3)], 1)
@@ -243,11 +243,13 @@
         if left != right:
             values.append(lr * ri - li * rr)
         for value in values:
-            out_ref[64 * place : 64 * place + 64, :] = dot_nn(jnp.concatenate(split(value), 1), select) * scale
+            sums = dot_nn(jnp.concatenate(split(value), 1), select) * scale
+            out_ref[64 * place : 64 * place + 64, :] = sums
+            packed_ref[32 * place : 32 * place + 32, :] = jnp.where(lane64[:32] < 64, sums[:32], sums[32:])
             place += 1
 
 
-def back_rows(core, banded_ref, back_ref, back_tw_ref):
+def back_rows(core, banded, back_ref, back_tw_ref):
     zeros = jnp.zeros((32, 128), F32)
     columns = []
     for k in range(2):
@@ -257,7 +259,7 @@
                 if part == 1 and left == right:
                     pieces.append(zeros)
                     continue
-                pieces.append(banded_ref[64 * place + 32 * k : 64 * place + 32 * k + 32, :])
+                pieces.append(banded[place][k])
                 place += 1
         for sp in range(3):
             columns.append(jnp.concatenate(pieces[4 * sp : 4 * sp + 4], 0))
@@ -278,14 +280,21 @@
 
 
 def middle_own_kernel(core, own_ref, back_ref, back_tw_ref, out_ref):
-    for py, block in enumerate(back_rows(core, own_ref, back_ref, back_tw_ref)):
+    banded = [[own_ref[64 * place + 32 * k : 64 * place + 32 * k + 32, :] for k in range(2)] for place in range(9)]
+    for py, block in enumerate(back_rows(core, banded, back_ref, back_tw_ref)):
         out_ref[96 * py : 96 * py + 96, :] = block
 
 
 def middle_back_kernel(core, rows_ref, got_ref, back_ref, back_tw_ref, final_ref, out_ref):
     first_core = core == 0
     lane = lax.broadcasted_iota(jnp.int32, (16, 128), 1)
-    for py, got in enumerate(back_rows(core, got_ref, back_ref, back_tw_ref)):
+    first_half = lax.broadcasted_iota(jnp.int32, (32, 128), 1) < 64
+    banded = []
+    for place in range(9):
+        packed = got_ref[32 * place : 32 * place + 32, :]
+        turned = pltpu.roll(packed, 64, axis=1)
+        banded.append((jnp.where(first_half, packed, turned), jnp.where(first_half, turned, packed)))
+    for py, got in enumerate(back_rows(core, banded, back_ref, back_tw_ref)):
         own = rows_ref[96 * py : 96 * py + 96, :]
         first = jnp.where(first_core, own, got)
         second = jnp.where(first_core, got, own)
@@ -355,12 +364,14 @@
 VMEM, HBM = pltpu.VMEM, pltpu.HBM
 
 
-def call(kernel, out_shape, in_specs, name, out_space=VMEM, scratch=(), dtype=F32):
+def call(kernel, out_shapes, in_specs, name, out_space=VMEM, scratch=(), dtype=F32):
+    shapes = [jax.ShapeDtypeStruct(shape, dtype) for shape in out_shapes]
+    out_specs = spaces(*[out_space] * len(shapes))
     return pl.pallas_call(
         kernel,
-        out_shape=jax.ShapeDtypeStruct(out_shape, dtype),
+        out_shape=shapes if len(shapes) > 1 else shapes[0],
         in_specs=in_specs,
-        out_specs=pl.BlockSpec(memory_space=out_space),
+        out_specs=out_specs if len(shapes) > 1 else out_specs[0],
         scratch_shapes=list(scratch),
         name=name,
         compiler_params=pltpu.CompilerParams(vmem_limit_bytes=16 * 1024 * 1024),
@@ -374,7 +385,7 @@
 def run_span_forward(velocity):
     twiddle, table = span_forward_tables()
     scratch = (VMEM((768, 128), F32), VMEM(twiddle.shape, F32), VMEM(table.shape, BF16), pltpu.SemaphoreType.DMA((3,)))
-    run = call(span_forward_kernel, (768, 128), spaces(HBM, HBM, HBM), "span_forward", scratch=scratch)
+    run = call(span_forward_kernel, [(768, 128)], spaces(HBM, HBM, HBM), "span_forward", scratch=scratch)
     return run(in_hbm(velocity), in_hbm(twiddle), in_hbm(table))
 
 
@@ -386,7 +397,7 @@
         middle_front_kernel(at_anchor, *refs)
 
     scratch = (pltpu.SMEM((8,), jnp.int32), pltpu.SemaphoreType.DMA)
-    run = call(kernel, (576, 128), spaces(HBM, *[VMEM] * 4), "middle_front", scratch=scratch)
+    run = call(kernel, [(576, 128), (288, 128)], spaces(HBM, *[VMEM] * 4), "middle_front", scratch=scratch)
     return run(in_hbm(band_of), received, *middle_tables()[0])
 
 
@@ -395,27 +406,27 @@
         middle_own_kernel(lax.axis_index("core") if core is None else core, *refs)
 
     back, twiddle, _ = middle_tables()[1]
-    return call(kernel, (768, 256), spaces(*[VMEM] * 3), "middle_own", dtype=BF16)(own, back, twiddle)
+    return call(kernel, [(768, 256)], spaces(*[VMEM] * 3), "middle_own", dtype=BF16)(own, back, twiddle)
 
 
 def run_middle_back(rows, got, core=None):
     def kernel(*refs):
         middle_back_kernel(lax.axis_index("core") if core is None else core, *refs)
 
-    return call(kernel, (384, 128), spaces(*[VMEM] * 5), "middle_back")(rows, got, *middle_tables()[1])
+    return call(kernel, [(384, 128)], spaces(*[VMEM] * 5), "middle_back")(rows, got, *middle_tables()[1])
 
 
 def run_span_inverse(received):
     scratch = (VMEM((384, 128), F32), pltpu.SemaphoreType.DMA((3,)))
-    run = call(span_inverse_kernel, (384, 128), spaces(VMEM, VMEM, VMEM), "span_inverse", HBM, scratch)
+    run = call(span_inverse_kernel, [(384, 128)], spaces(VMEM, VMEM, VMEM), "span_inverse", HBM, scratch)
     return run(received, *span_inverse_tables())
 
 
 def per_device(velocity, band_of):
     sent = run_span_forward(velocity.reshape(768, 128))
     received = lax.all_to_all(sent.reshape(256, 1, 384), FRONT_AXES, 0, 0, tiled=True)
-    own = run_middle_front(received.reshape(768, 128), band_of)
-    got = lax.ppermute(own, "core", ((0, 1), (1, 0)))
+    own, packed = run_middle_front(received.reshape(768, 128), band_of)
+    got = lax.ppermute(packed, "core", ((0, 1), (1, 0)))
     back = run_middle_back(run_middle_own(own), got)
     gathered = lax.all_to_all(back.reshape(128, 1, 384), BACK_AXES, 0, 0, tiled=True)
     out = run_span_inverse(gathered.reshape(384, 128))

time: 57.4 us -> 57.3 us (level)
  no operation moved by 1% of the time
where the time goes in v9:
time: 57.3 us; the launch traced here: 56.5 us
  blocking collectives  49.5 us (86%)
  Pallas kernels  5.06 us (9%)
  starting transfers between devices  1.14 us (2%)
  waiting for transfers between devices  0.7 us (1%)
    all_to_all x1, blocking collectives, per_device(): lax.all_to_all(sent.reshape(256, 1, 384), FRONT_AXES, 0, 0, tiled=True)  32.5 us
    all_to_all x1, blocking collectives, per_device(): lax.all_to_all(back.reshape(128, 1, 384), BACK_AXES, 0, 0, tiled=True)  16.9 us
    pallas_call x1, Pallas kernels, run_span_forward(): return run(in_hbm(velocity), in_hbm(twiddle), in_hbm(table))  1.7 us
    pallas_call x1, Pallas kernels, run_middle_front(): return run(in_hbm(band_of), received, *middle_tables()[0])  1.17 us
  transfers between devices with their start and end apart: 1, of which 1 were waited for; matrix products, arithmetic and copies ran while one was open for 0% of the time, Pallas kernels for 1%

profile of v9, /device:TPU:1, one launch (start us, length us, event | category | flops | bytes accessed | tf_op | source)
XLA Modules:
  0.0 56.5 jit_solution(12307135192658111023)
XLA Ops:
  0.0 0.0 copy-start.4
  0.0 1.7 %span_forward.1 = f32[768,128]{1,0:T(8,128)S(1)} custom-call(f32[768,128]{1,0:T(8,128)} %bitcast.14, f32[16,128]{1,0:T(8,128)} %constant.18.clone.twiddle_hbm.twiddle_ref, bf16[128,256]{1,0:T(8,128)(2,1)} %constant.19.clone.table_hbm), custom_call_target="tpu_custom_call" | custom-call | tf_op jit(solution)/shard_map/span_forward/pallas_call | solution.py:389
  1.7 0.0 copy-start
  1.7 0.0 copy-start.5
  1.7 32.5 %all_to_all.10 = f32[256,1,384]{2,1,0:T(1,128)S(1)} all-to-all(f32[256,1,384]{2,1,0:T(1,128)S(1)} %bitcast.11), channel_id=1, replica_groups=mesh['x'=4,'zh'=4,'core'=2,'zl'=2,'y'=4] {'zh','zl','y','x','core'}, dimensions={0} | all-to-all | bytes 786432 | tf_op jit(solution)/shard_map/all_to_all | solution.py:427
  34.3 0.0 copy-done.4
  34.3 0.0 copy-done
  34.3 0.0 copy-done.5
  34.3 0.0 copy-start.1
  34.3 0.0 copy-start.2
  34.3 1.2 %middle_front.1 = (f32[576,128]{1,0:T(8,128)S(1)}, f32[288,128]{1,0:T(8,128)S(1)}) custom-call(s32[8]{0:T(128)} %refs_0_.1, f32[768,128]{1,0:T(8,128)S(1)} %bitcast.10, bf16[256,768]{1,0:T(8,128)(2,1)S(1)} %copy-done.4, f32[1024,128]{1,0:T(8,128)S(1)} %copy-done, bf16[256,256]{1,0:T(8,128)(2,1)S(1)} %copy-done.5), custom_call_target="tpu_custom_call" | custom-call | tf_op jit(solution)/shard_map/middle_front/pallas_call | solution.py:401
  35.5 1.1 %collective-permute-start = (f32[288,128]{1,0:T(8,128)S(1)}, f32[288,128]{1,0:T(8,128)S(1)}, u32[]{:S(2)}, u32[]{:S(2)}) collective-permute-start(f32[288,128]{1,0:T(8,128)S(1)} %get-tuple-element.8), channel_id=1, source_target_pairs={{0,8},{8,0},{1,9},{9,1},{2,10},{10,2},{3,11},{11,3},{4,12},{12,4},... | collective-permute-start | bytes 442376 | tf_op jit(solution)/shard_map/ppermute | solution.py:429
  36.6 0.0 copy-done.1
  36.6 0.0 copy-done.2
  36.6 0.0 copy-start.7
  36.6 0.3 middle_own.1.refs_0_
  36.9 0.7 %collective-permute-done.refs_1_ = f32[288,128]{1,0:T(8,128)S(1)} collective-permute-done((f32[288,128]{1,0:T(8,128)S(1)}, f32[288,128]{1,0:T(8,128)S(1)}, u32[]{:S(2)}, u32[]{:S(2)}) %collective-permute-start) | collective-permute-done | bytes 147488 | tf_op jit(solution)/shard_map/ppermute | solution.py:429
  37.6 0.0 copy-done.7
  37.6 0.0 copy-start.6
  37.6 0.8 %middle_back.1 = f32[384,128]{1,0:T(8,128)S(1)} custom-call(bf16[768,256]{1,0:T(8,128)(2,1)S(1)} %middle_own.1.refs_0_, f32[288,128]{1,0:T(8,128)S(1)} %collective-permute-done.refs_1_, bf16[256,256]{1,0:T(8,128)(2,1)S(1)} %copy-done.2, f32[256,128]{1,0:T(8,128)S(1)} %copy-done.1, bf16[64,256]{1,0:T(8,128)(2,1)S(1)} %copy-done.7), custom_call_target="tpu_custom_call" | custom-call | tf_op jit(solution)/shard_map/middle_back/pallas_call | solution.py:416
  38.4 0.0 copy-start.3
  38.4 16.9 %all_to_all.11 = f32[128,1,384]{2,1,0:T(1,128)S(1)} all-to-all(f32[128,1,384]{2,1,0:T(1,128)S(1)} %bitcast.13), channel_id=1, replica_groups=mesh['x'=4,'zh'=4,'core'=2,'zl'=2,'y'=4] {'zl','y','zh','x'}, dimensions={0} | all-to-all | bytes 393216 | tf_op jit(solution)/shard_map/all_to_all | solution.py:431
  55.4 0.0 copy-done.6
  55.4 0.0 copy-done.3
  55.4 1.1 %span_inverse.1 = f32[384,128]{1,0:T(8,128)} custom-call(f32[384,128]{1,0:T(8,128)S(1)} %bitcast.12, bf16[384,512]{1,0:T(8,128)(2,1)S(1)} %copy-done.3, f32[16,128]{1,0:T(8,128)S(1)} %copy-done.6), custom_call_target="tpu_custom_call" | custom-call | tf_op jit(solution)/shard_map/span_inverse/pallas_call | solution.py:422
Async XLA Ops:
  0.0 34.3 %copy-start.4 = (bf16[256,768]{1,0:T(8,128)(2,1)S(1)}, bf16[256,768]{1,0:T(8,128)(2,1)}, u32[]{:S(2)}) copy-start(bf16[256,768]{1,0:T(8,128)(2,1)} %constant.20.clone.refs_2_) | copy-start | bytes 1179652
  1.7 32.6 %copy-start = (f32[1024,128]{1,0:T(8,128)S(1)}, f32[1024,128]{1,0:T(8,128)}, u32[]{:S(2)}) copy-start(f32[1024,128]{1,0:T(8,128)} %constant.21.clone.refs_3_) | copy-start | bytes 1572868
  1.7 32.6 %copy-start.5 = (bf16[256,256]{1,0:T(8,128)(2,1)S(1)}, bf16[256,256]{1,0:T(8,128)(2,1)}, u32[]{:S(2)}) copy-start(bf16[256,256]{1,0:T(8,128)(2,1)} %constant.22.clone.refs_4_) | copy-start | bytes 393220
  34.3 2.3 %copy-start.1 = (f32[256,128]{1,0:T(8,128)S(1)}, f32[256,128]{1,0:T(8,128)}, u32[]{:S(2)}) copy-start(f32[256,128]{1,0:T(8,128)} %constant.24.clone.refs_2_.refs_3_) | copy-start | bytes 393220
  34.3 2.3 %copy-start.2 = (bf16[256,256]{1,0:T(8,128)(2,1)S(1)}, bf16[256,256]{1,0:T(8,128)(2,1)}, u32[]{:S(2)}) copy-start(bf16[256,256]{1,0:T(8,128)(2,1)} %constant.23.clone.refs_1_.refs_2_) | copy-start | bytes 393220
  35.5 2.1 %collective-permute-start = (f32[288,128]{1,0:T(8,128)S(1)}, f32[288,128]{1,0:T(8,128)S(1)}, u32[]{:S(2)}, u32[]{:S(2)}) collective-permute-start(f32[288,128]{1,0:T(8,128)S(1)} %get-tuple-element.8), channel_id=1, source_target_pairs={{0,8},{8,0},{1,9},{9,1},{2,10},{10,2},{3,11},{11,3},{4,12},{12,4},... | collective-permute-start | bytes 442376 | tf_op jit(solution)/shard_map/ppermute | solution.py:429
  36.6 1.0 %copy-start.7 = (bf16[64,256]{1,0:T(8,128)(2,1)S(1)}, bf16[64,256]{1,0:T(8,128)(2,1)}, u32[]{:S(2)}) copy-start(bf16[64,256]{1,0:T(8,128)(2,1)} %constant.25.clone.refs_4_) | copy-start | bytes 98308
  37.6 17.7 %copy-start.6 = (f32[16,128]{1,0:T(8,128)S(1)}, f32[16,128]{1,0:T(8,128)}, u32[]{:S(2)}) copy-start(f32[16,128]{1,0:T(8,128)} %constant.18.clone.twiddle_hbm.twiddle_ref) | copy-start | bytes 24580
  38.4 17.0 %copy-start.3 = (bf16[384,512]{1,0:T(8,128)(2,1)S(1)}, bf16[384,512]{1,0:T(8,128)(2,1)}, u32[]{:S(2)}) copy-start(bf16[384,512]{1,0:T(8,128)(2,1)} %constant.26.clone.table_ref) | copy-start | bytes 1179652

commit v10 on v9

--- a/solution.py
+++ b/solution.py
@@ -40,10 +40,10 @@
     places = np.indices([sizes[axis] for axis in axes]).reshape(len(axes), -1)
     at = dict(zip(axes, places))
     px = (at["x"] * 4 + at["zh"]) * 2 + at.get("core", 0)
-    return px, at["zl"] * 4 + at["y"], ((at["zh"] * 2 + at["zl"]) * 4 + at["y"]) * 4 + at["x"]
-
-
-FRONT_AXES = ("zh", "zl", "y", "x", "core")
+    return px, at["zl"] * 4 + at["y"], ((at["x"] * 4 + at["zh"]) * 2 + at["zl"]) * 4 + at["y"]
+
+
+FRONT_AXES = ("zh", "zl", "y", "core", "x")
 BACK_AXES = ("zl", "y", "zh", "x")
 
 
@@ -187,8 +187,9 @@
             columns.append(jnp.concatenate(rows, 0))
         result = halves_added(dot_nt(table, columns[0])) + dot_nt(table[:64], columns[1])
         for c in range(3):
-            first = 384 * (j // 2) + 3 * (j % 2) + c
-            out_ref[pl.ds(first, 64, stride=6), :] = result[:, 128 * c : 128 * c + 128]
+            for half in range(2):
+                first = 3 * (4 * (j % 2) + 2 * (j // 2) + half) + c
+                out_ref[pl.ds(first, 32, stride=24), :] = result[32 * half : 32 * half + 32, 128 * c : 128 * c + 128]
 
 
 def middle_front_kernel(anchor, band_hbm, r_ref, over_px_ref, front_tw_ref, within_ref, out_ref, packed_ref, band_ref, sem):

time: 57.3 us -> 57.4 us (level)
  starting transfers between devices: 1.14 us -> 0.09 us
  blocking collectives: 49.5 us -> 50.3 us
    ppermute x1, starting transfers between devices: 1.14 us -> 0.09 us  [per_device(): got = lax.ppermute(packed, 'core', ((0, 1), (1, 0)))]
    all_to_all x1, blocking collectives: 16.9 us -> 17.6 us  [per_device(): lax.all_to_all(back.reshape(128, 1, 384), BACK_AXES, 0, 0, tiled=True)]
where the time goes in v10:
time: 57.4 us; the launch traced here: 56.7 us
  blocking collectives  50.3 us (88%)
  Pallas kernels  5.07 us (9%)
  waiting for transfers between devices  1.02 us (2%)
    all_to_all x1, blocking collectives, per_device(): lax.all_to_all(sent.reshape(256, 1, 384), FRONT_AXES, 0, 0, tiled=True)  32.8 us
    all_to_all x1, blocking collectives, per_device(): lax.all_to_all(back.reshape(128, 1, 384), BACK_AXES, 0, 0, tiled=True)  17.6 us
    pallas_call x1, Pallas kernels, run_span_forward(): return run(in_hbm(velocity), in_hbm(twiddle), in_hbm(table))  1.71 us
    pallas_call x1, Pallas kernels, run_middle_front(): return run(in_hbm(band_of), received, *middle_tables()[0])  1.17 us
  transfers between devices with their start and end apart: 1, of which 1 were waited for; matrix products, arithmetic and copies ran while one was open for 0% of the time, Pallas kernels for 1%

profile of v10, /device:TPU:1, one launch (start us, length us, event | category | flops | bytes accessed | tf_op | source)
XLA Modules:
  0.0 56.7 jit_solution(5964311228752634433)
XLA Ops:
  0.0 0.0 copy-start.4
  0.0 1.7 %span_forward.1 = f32[768,128]{1,0:T(8,128)S(1)} custom-call(f32[768,128]{1,0:T(8,128)} %bitcast.14, f32[16,128]{1,0:T(8,128)} %constant.18.clone.twiddle_hbm.twiddle_ref, bf16[128,256]{1,0:T(8,128)(2,1)} %constant.19.clone.table_hbm), custom_call_target="tpu_custom_call" | custom-call | tf_op jit(solution)/shard_map/span_forward/pallas_call | solution.py:390
  1.7 0.0 copy-start
  1.7 0.0 copy-start.5
  1.7 32.8 %all_to_all.10 = f32[256,1,384]{2,1,0:T(1,128)S(1)} all-to-all(f32[256,1,384]{2,1,0:T(1,128)S(1)} %bitcast.11), channel_id=1, replica_groups=mesh['x'=4,'zh'=4,'core'=2,'zl'=2,'y'=4] {'zh','zl','y','core','x'}, dimensions={0} | all-to-all | bytes 786432 | tf_op jit(solution)/shard_map/all_to_all | solution.py:428
  34.5 0.0 copy-done.4
  34.5 0.0 copy-done
  34.5 0.0 copy-done.5
  34.5 0.0 copy-start.1
  34.5 0.0 copy-start.2
  34.5 1.2 %middle_front.1 = (f32[576,128]{1,0:T(8,128)S(1)}, f32[288,128]{1,0:T(8,128)S(1)}) custom-call(s32[8]{0:T(128)} %refs_0_.1, f32[768,128]{1,0:T(8,128)S(1)} %bitcast.10, bf16[256,768]{1,0:T(8,128)(2,1)S(1)} %copy-done.4, f32[1024,128]{1,0:T(8,128)S(1)} %copy-done, bf16[256,256]{1,0:T(8,128)(2,1)S(1)} %copy-done.5), custom_call_target="tpu_custom_call" | custom-call | tf_op jit(solution)/shard_map/middle_front/pallas_call | solution.py:402
  35.7 0.1 collective-permute-start
  35.8 0.0 copy-done.1
  35.8 0.0 copy-done.2
  35.8 0.0 copy-start.7
  35.8 0.3 middle_own.1.refs_0_
  36.1 1.0 %collective-permute-done.refs_1_ = f32[288,128]{1,0:T(8,128)S(1)} collective-permute-done((f32[288,128]{1,0:T(8,128)S(1)}, f32[288,128]{1,0:T(8,128)S(1)}, u32[]{:S(2)}, u32[]{:S(2)}) %collective-permute-start) | collective-permute-done | bytes 147488 | tf_op jit(solution)/shard_map/ppermute | solution.py:430
  37.2 0.0 copy-done.7
  37.2 0.0 copy-start.6
  37.2 0.8 %middle_back.1 = f32[384,128]{1,0:T(8,128)S(1)} custom-call(bf16[768,256]{1,0:T(8,128)(2,1)S(1)} %middle_own.1.refs_0_, f32[288,128]{1,0:T(8,128)S(1)} %collective-permute-done.refs_1_, bf16[256,256]{1,0:T(8,128)(2,1)S(1)} %copy-done.2, f32[256,128]{1,0:T(8,128)S(1)} %copy-done.1, bf16[64,256]{1,0:T(8,128)(2,1)S(1)} %copy-done.7), custom_call_target="tpu_custom_call" | custom-call | tf_op jit(solution)/shard_map/middle_back/pallas_call | solution.py:417
  37.9 0.0 copy-start.3
  38.0 17.6 %all_to_all.11 = f32[128,1,384]{2,1,0:T(1,128)S(1)} all-to-all(f32[128,1,384]{2,1,0:T(1,128)S(1)} %bitcast.13), channel_id=1, replica_groups=mesh['x'=4,'zh'=4,'core'=2,'zl'=2,'y'=4] {'zl','y','zh','x'}, dimensions={0} | all-to-all | bytes 393216 | tf_op jit(solution)/shard_map/all_to_all | solution.py:432
  55.5 0.0 copy-done.6
  55.6 0.0 copy-done.3
  55.6 1.1 %span_inverse.1 = f32[384,128]{1,0:T(8,128)} custom-call(f32[384,128]{1,0:T(8,128)S(1)} %bitcast.12, bf16[384,512]{1,0:T(8,128)(2,1)S(1)} %copy-done.3, f32[16,128]{1,0:T(8,128)S(1)} %copy-done.6), custom_call_target="tpu_custom_call" | custom-call | tf_op jit(solution)/shard_map/span_inverse/pallas_call | solution.py:423
Async XLA Ops:
  0.0 34.5 %copy-start.4 = (bf16[256,768]{1,0:T(8,128)(2,1)S(1)}, bf16[256,768]{1,0:T(8,128)(2,1)}, u32[]{:S(2)}) copy-start(bf16[256,768]{1,0:T(8,128)(2,1)} %constant.20.clone.refs_2_) | copy-start | bytes 1179652
  1.7 32.8 %copy-start = (f32[1024,128]{1,0:T(8,128)S(1)}, f32[1024,128]{1,0:T(8,128)}, u32[]{:S(2)}) copy-start(f32[1024,128]{1,0:T(8,128)} %constant.21.clone.refs_3_) | copy-start | bytes 1572868
  1.7 32.8 %copy-start.5 = (bf16[256,256]{1,0:T(8,128)(2,1)S(1)}, bf16[256,256]{1,0:T(8,128)(2,1)}, u32[]{:S(2)}) copy-start(bf16[256,256]{1,0:T(8,128)(2,1)} %constant.22.clone.refs_4_) | copy-start | bytes 393220
  34.5 1.3 %copy-start.1 = (f32[256,128]{1,0:T(8,128)S(1)}, f32[256,128]{1,0:T(8,128)}, u32[]{:S(2)}) copy-start(f32[256,128]{1,0:T(8,128)} %constant.24.clone.refs_2_.refs_3_) | copy-start | bytes 393220
  34.5 1.3 %copy-start.2 = (bf16[256,256]{1,0:T(8,128)(2,1)S(1)}, bf16[256,256]{1,0:T(8,128)(2,1)}, u32[]{:S(2)}) copy-start(bf16[256,256]{1,0:T(8,128)(2,1)} %constant.23.clone.refs_1_.refs_2_) | copy-start | bytes 393220
  35.7 1.5 %collective-permute-start = (f32[288,128]{1,0:T(8,128)S(1)}, f32[288,128]{1,0:T(8,128)S(1)}, u32[]{:S(2)}, u32[]{:S(2)}) collective-permute-start(f32[288,128]{1,0:T(8,128)S(1)} %get-tuple-element.8), channel_id=1, source_target_pairs={{0,8},{8,0},{1,9},{9,1},{2,10},{10,2},{3,11},{11,3},{4,12},{12,4},... | collective-permute-start | bytes 442376 | tf_op jit(solution)/shard_map/ppermute | solution.py:430
  35.8 1.3 %copy-start.7 = (bf16[64,256]{1,0:T(8,128)(2,1)S(1)}, bf16[64,256]{1,0:T(8,128)(2,1)}, u32[]{:S(2)}) copy-start(bf16[64,256]{1,0:T(8,128)(2,1)} %constant.25.clone.refs_4_) | copy-start | bytes 98308
  37.2 18.4 %copy-start.6 = (f32[16,128]{1,0:T(8,128)S(1)}, f32[16,128]{1,0:T(8,128)}, u32[]{:S(2)}) copy-start(f32[16,128]{1,0:T(8,128)} %constant.18.clone.twiddle_hbm.twiddle_ref) | copy-start | bytes 24580
  37.9 17.6 %copy-start.3 = (bf16[384,512]{1,0:T(8,128)(2,1)S(1)}, bf16[384,512]{1,0:T(8,128)(2,1)}, u32[]{:S(2)}) copy-start(bf16[384,512]{1,0:T(8,128)(2,1)} %constant.26.clone.table_ref) | copy-start | bytes 1179652

commit v11 on v9

--- a/solution.py
+++ b/solution.py
@@ -350,9 +350,10 @@
                 base = (sp * 2 * 2 + b) * 32 + half * 8
                 out_ref[pl.ds(base, 8), :] = jnp.where(sub < 4, v0, pltpu.roll(v1, 4, axis=0))
                 out_ref[pl.ds(base + 64, 8), :] = jnp.where(sub < 4, pltpu.roll(v0, 4, axis=0), v1)
-        block = pl.ds(128 * sp, 128)
-        copies.append(pltpu.make_async_copy(out_ref.at[block], out_hbm.at[block], sems.at[sp]))
-        copies[-1].start()
+            for second in range(2):
+                block = pl.ds(32 * (4 * sp + 2 * second + b), 32)
+                copies.append(pltpu.make_async_copy(out_ref.at[block], out_hbm.at[block], sems.at[len(copies)]))
+                copies[-1].start()
     for copy in copies:
         copy.wait()
 
@@ -417,7 +418,7 @@
 
 
 def run_span_inverse(received):
-    scratch = (VMEM((384, 128), F32), pltpu.SemaphoreType.DMA((3,)))
+    scratch = (VMEM((384, 128), F32), pltpu.SemaphoreType.DMA((12,)))
     run = call(span_inverse_kernel, [(384, 128)], spaces(VMEM, VMEM, VMEM), "span_inverse", HBM, scratch)
     return run(received, *span_inverse_tables())
 

time: 57.3 us -> 57.3 us (level)
  no operation moved by 1% of the time
where the time goes in v11:
time: 57.3 us; the launch traced here: 56.6 us
  blocking collectives  49.5 us (86%)
  Pallas kernels  5.12 us (9%)
  starting transfers between devices  1.14 us (2%)
  waiting for transfers between devices  0.7 us (1%)
    all_to_all x1, blocking collectives, per_device(): lax.all_to_all(sent.reshape(256, 1, 384), FRONT_AXES, 0, 0, tiled=True)  32.5 us
    all_to_all x1, blocking collectives, per_device(): lax.all_to_all(back.reshape(128, 1, 384), BACK_AXES, 0, 0, tiled=True)  16.9 us
    pallas_call x1, Pallas kernels, run_span_forward(): return run(in_hbm(velocity), in_hbm(twiddle), in_hbm(table))  1.7 us
    pallas_call x1, Pallas kernels, run_span_inverse(): return run(received, *span_inverse_tables())  1.19 us
    pallas_call x1, Pallas kernels, run_middle_front(): return run(in_hbm(band_of), received, *middle_tables()[0])  1.17 us
  transfers between devices with their start and end apart: 1, of which 1 were waited for; matrix products, arithmetic and copies ran while one was open for 0% of the time, Pallas kernels for 1%

profile of v11, /device:TPU:1, one launch (start us, length us, event | category | flops | bytes accessed | tf_op | source)
XLA Modules:
  0.0 56.6 jit_solution(12921730244796864637)
XLA Ops:
  0.0 0.0 copy-start.4
  0.0 1.7 %span_forward.1 = f32[768,128]{1,0:T(8,128)S(1)} custom-call(f32[768,128]{1,0:T(8,128)} %bitcast.14, f32[16,128]{1,0:T(8,128)} %constant.18.clone.twiddle_hbm.twiddle_ref, bf16[128,256]{1,0:T(8,128)(2,1)} %constant.19.clone.table_hbm), custom_call_target="tpu_custom_call" | custom-call | tf_op jit(solution)/shard_map/span_forward/pallas_call | solution.py:390
  1.7 0.0 copy-start
  1.7 0.0 copy-start.5
  1.7 32.5 %all_to_all.10 = f32[256,1,384]{2,1,0:T(1,128)S(1)} all-to-all(f32[256,1,384]{2,1,0:T(1,128)S(1)} %bitcast.11), channel_id=1, replica_groups=mesh['x'=4,'zh'=4,'core'=2,'zl'=2,'y'=4] {'zh','zl','y','x','core'}, dimensions={0} | all-to-all | bytes 786432 | tf_op jit(solution)/shard_map/all_to_all | solution.py:428
  34.3 0.0 copy-done.4
  34.3 0.0 copy-done
  34.3 0.0 copy-done.5
  34.3 0.0 copy-start.1
  34.3 0.0 copy-start.2
  34.3 1.2 %middle_front.1 = (f32[576,128]{1,0:T(8,128)S(1)}, f32[288,128]{1,0:T(8,128)S(1)}) custom-call(s32[8]{0:T(128)} %refs_0_.1, f32[768,128]{1,0:T(8,128)S(1)} %bitcast.10, bf16[256,768]{1,0:T(8,128)(2,1)S(1)} %copy-done.4, f32[1024,128]{1,0:T(8,128)S(1)} %copy-done, bf16[256,256]{1,0:T(8,128)(2,1)S(1)} %copy-done.5), custom_call_target="tpu_custom_call" | custom-call | tf_op jit(solution)/shard_map/middle_front/pallas_call | solution.py:402
  35.5 1.1 %collective-permute-start = (f32[288,128]{1,0:T(8,128)S(1)}, f32[288,128]{1,0:T(8,128)S(1)}, u32[]{:S(2)}, u32[]{:S(2)}) collective-permute-start(f32[288,128]{1,0:T(8,128)S(1)} %get-tuple-element.8), channel_id=1, source_target_pairs={{0,8},{8,0},{1,9},{9,1},{2,10},{10,2},{3,11},{11,3},{4,12},{12,4},... | collective-permute-start | bytes 442376 | tf_op jit(solution)/shard_map/ppermute | solution.py:430
  36.6 0.0 copy-done.1
  36.6 0.0 copy-done.2
  36.6 0.0 copy-start.7
  36.6 0.3 middle_own.1.refs_0_
  36.9 0.7 %collective-permute-done.refs_1_ = f32[288,128]{1,0:T(8,128)S(1)} collective-permute-done((f32[288,128]{1,0:T(8,128)S(1)}, f32[288,128]{1,0:T(8,128)S(1)}, u32[]{:S(2)}, u32[]{:S(2)}) %collective-permute-start) | collective-permute-done | bytes 147488 | tf_op jit(solution)/shard_map/ppermute | solution.py:430
  37.6 0.0 copy-done.7
  37.6 0.0 copy-start.6
  37.6 0.8 %middle_back.1 = f32[384,128]{1,0:T(8,128)S(1)} custom-call(bf16[768,256]{1,0:T(8,128)(2,1)S(1)} %middle_own.1.refs_0_, f32[288,128]{1,0:T(8,128)S(1)} %collective-permute-done.refs_1_, bf16[256,256]{1,0:T(8,128)(2,1)S(1)} %copy-done.2, f32[256,128]{1,0:T(8,128)S(1)} %copy-done.1, bf16[64,256]{1,0:T(8,128)(2,1)S(1)} %copy-done.7), custom_call_target="tpu_custom_call" | custom-call | tf_op jit(solution)/shard_map/middle_back/pallas_call | solution.py:417
  38.4 0.0 copy-start.3
  38.4 16.9 %all_to_all.11 = f32[128,1,384]{2,1,0:T(1,128)S(1)} all-to-all(f32[128,1,384]{2,1,0:T(1,128)S(1)} %bitcast.13), channel_id=1, replica_groups=mesh['x'=4,'zh'=4,'core'=2,'zl'=2,'y'=4] {'zl','y','zh','x'}, dimensions={0} | all-to-all | bytes 393216 | tf_op jit(solution)/shard_map/all_to_all | solution.py:432
  55.4 0.0 copy-done.6
  55.4 0.0 copy-done.3
  55.4 1.2 %span_inverse.1 = f32[384,128]{1,0:T(8,128)} custom-call(f32[384,128]{1,0:T(8,128)S(1)} %bitcast.12, bf16[384,512]{1,0:T(8,128)(2,1)S(1)} %copy-done.3, f32[16,128]{1,0:T(8,128)S(1)} %copy-done.6), custom_call_target="tpu_custom_call" | custom-call | tf_op jit(solution)/shard_map/span_inverse/pallas_call | solution.py:423
Async XLA Ops:
  0.0 34.3 %copy-start.4 = (bf16[256,768]{1,0:T(8,128)(2,1)S(1)}, bf16[256,768]{1,0:T(8,128)(2,1)}, u32[]{:S(2)}) copy-start(bf16[256,768]{1,0:T(8,128)(2,1)} %constant.20.clone.refs_2_) | copy-start | bytes 1179652
  1.7 32.6 %copy-start = (f32[1024,128]{1,0:T(8,128)S(1)}, f32[1024,128]{1,0:T(8,128)}, u32[]{:S(2)}) copy-start(f32[1024,128]{1,0:T(8,128)} %constant.21.clone.refs_3_) | copy-start | bytes 1572868
  1.7 32.6 %copy-start.5 = (bf16[256,256]{1,0:T(8,128)(2,1)S(1)}, bf16[256,256]{1,0:T(8,128)(2,1)}, u32[]{:S(2)}) copy-start(bf16[256,256]{1,0:T(8,128)(2,1)} %constant.22.clone.refs_4_) | copy-start | bytes 393220
  34.3 2.3 %copy-start.1 = (f32[256,128]{1,0:T(8,128)S(1)}, f32[256,128]{1,0:T(8,128)}, u32[]{:S(2)}) copy-start(f32[256,128]{1,0:T(8,128)} %constant.24.clone.refs_2_.refs_3_) | copy-start | bytes 393220
  34.3 2.3 %copy-start.2 = (bf16[256,256]{1,0:T(8,128)(2,1)S(1)}, bf16[256,256]{1,0:T(8,128)(2,1)}, u32[]{:S(2)}) copy-start(bf16[256,256]{1,0:T(8,128)(2,1)} %constant.23.clone.refs_1_.refs_2_) | copy-start | bytes 393220
  35.5 2.1 %collective-permute-start = (f32[288,128]{1,0:T(8,128)S(1)}, f32[288,128]{1,0:T(8,128)S(1)}, u32[]{:S(2)}, u32[]{:S(2)}) collective-permute-start(f32[288,128]{1,0:T(8,128)S(1)} %get-tuple-element.8), channel_id=1, source_target_pairs={{0,8},{8,0},{1,9},{9,1},{2,10},{10,2},{3,11},{11,3},{4,12},{12,4},... | collective-permute-start | bytes 442376 | tf_op jit(solution)/shard_map/ppermute | solution.py:430
  36.6 1.0 %copy-start.7 = (bf16[64,256]{1,0:T(8,128)(2,1)S(1)}, bf16[64,256]{1,0:T(8,128)(2,1)}, u32[]{:S(2)}) copy-start(bf16[64,256]{1,0:T(8,128)(2,1)} %constant.25.clone.refs_4_) | copy-start | bytes 98308
  37.6 17.7 %copy-start.6 = (f32[16,128]{1,0:T(8,128)S(1)}, f32[16,128]{1,0:T(8,128)}, u32[]{:S(2)}) copy-start(f32[16,128]{1,0:T(8,128)} %constant.18.clone.twiddle_hbm.twiddle_ref) | copy-start | bytes 24580
  38.4 17.0 %copy-start.3 = (bf16[384,512]{1,0:T(8,128)(2,1)S(1)}, bf16[384,512]{1,0:T(8,128)(2,1)}, u32[]{:S(2)}) copy-start(bf16[384,512]{1,0:T(8,128)(2,1)} %constant.26.clone.table_ref) | copy-start | bytes 1179652
